TPU v7x, 256 devices: a whole 4x4x8 slice. The times are simulated.
256 devices in a mesh: grp: 8 (over z_hi, x), tile: 32 (over z_lo, y, core).
Axes of the slice: x: 4, y: 4, z: 8 (z_hi: 2, z_lo: 4; z = z_hi * 4 + z_lo), core: 2. Of those that a mesh axis runs over, the one named last changes fastest.
Arguments:
- visibility: bfloat16 [2, 512, 512, 1024], P(None, 'tile', None, 'grp'), may hold values from -3 to 3, as said below
- dish_pair_okay: int32 [512, 512], P('tile'), may hold values 0 or 1
- triangles: int32 [3, 65536], P(None, 'tile'), may hold values from 0 to 511, as said below
Outputs:
- triangle_means: float32 [2, 65536], P(None, 'tile')
- closure_spectrum: float32 [2, 1024], P(None, ('grp', 'tile'))
Inputs may be any that keep to these rules, and one draw needn't show every extreme that they name: Both parts of every visibility lie in -3 to 3. `triangles`: column j belongs to block d = j // 2048 and level k = (j % 2048) // 1024; its first antenna lies in block d (antennas d * 16 to d * 16 + 15), its second in block d XOR 2**k, and its third is any antenna other than the first two.
All inputs are finite; a program needn't handle non-finite values. No bound on the sum of `dish_pair_okay` on one device may be relied on, other than what follows from the above.
Results may differ from a plain program's by a relative error of at most 0.0003.
Values may be sent and summed in bfloat16 or wider, within the bound.
A program may use at most 64 MiB of HBM per device.

v0:
```python
import jax
import jax.numpy as jnp
from jax import lax
from jax.sharding import PartitionSpec as P

RADIO_BANDS = 1024
LEVELS = 2
TRI_LVL = 1024


def swapped(array, axis, stride):
    return lax.ppermute(array, axis, [(i, i ^ 1 << stride) for i in range(lax.axis_size(axis))])


def copy_for_each(array, axis):
    devices = lax.axis_size(axis)
    return lax.all_to_all(
        jnp.broadcast_to(array[None], (devices, *array.shape)), axis, 0, 0, tiled=True
    )


def taken_together(array, axis):
    everything = copy_for_each(array, axis)
    return jnp.sum(everything, axis=0)


def split_up(array, dim, devices):
    dims = array.shape
    parts = array.reshape(*dims[:dim], devices, dims[dim] // devices, *dims[dim + 1 :])
    return jnp.moveaxis(parts, dim, 0)


def sum_at_owner(array, axis, dim):
    parts = split_up(array, dim, lax.axis_size(axis))
    arrived = lax.all_to_all(parts, axis, split_axis=0, concat_axis=0, tiled=True)
    return arrived.sum(axis=0)


def bispectrum(edge_ab, edge_bc, edge_ac):
    edge_ab = edge_ab.astype(jnp.float32)
    edge_bc = edge_bc.astype(jnp.float32)
    edge_ac = edge_ac.astype(jnp.float32)
    prod_real = edge_ab[0] * edge_bc[0] - edge_ab[1] * edge_bc[1]
    prod_imag = edge_ab[0] * edge_bc[1] + edge_ab[1] * edge_bc[0]
    real_part = prod_real * edge_ac[0] + prod_imag * edge_ac[1]
    imag_part = prod_imag * edge_ac[0] - prod_real * edge_ac[1]
    return (real_part, imag_part)


def pick_pairs(table, flag_table, row_index, col_index):
    dish_rows = table.shape[1]
    dish_cols = table.shape[2]
    channels = table.shape[3]
    planes = table.reshape(2, dish_rows * dish_cols, channels)
    flag_flat = flag_table.reshape(dish_rows * dish_cols)
    flat_index = row_index * dish_cols + col_index
    edges = jnp.take(planes, flat_index, axis=1)
    flags = jnp.take(flag_flat, flat_index, axis=0).astype(jnp.float32)
    return (edges, flags)


def body(visibility, dish_pair_okay, triangles):
    block_rows = visibility.shape[1]
    device = lax.axis_index("tile")
    flag_values = dish_pair_okay.astype(jnp.bfloat16)
    spec_real = jnp.zeros((visibility.shape[3],), jnp.float32)
    spec_imag = jnp.zeros((visibility.shape[3],), jnp.float32)
    spec_norm = jnp.zeros((visibility.shape[3],), jnp.float32)
    level_sums = [None] * LEVELS
    level_order = list(range(LEVELS))
    for level_bit in level_order:
        block = triangles[:, level_bit * TRI_LVL : (level_bit + 1) * TRI_LVL]
        count = block.shape[1]
        partner = jnp.bitwise_xor(device, 1 << level_bit)
        first_local = block[0] - device * block_rows
        second_local = block[1] - partner * block_rows
        vertex_point = block[2]
        own_edges, own_flags = pick_pairs(
            visibility,
            flag_values,
            jnp.concatenate([first_local, first_local]),
            jnp.concatenate([block[1], vertex_point]),
        )
        edge_ab = own_edges[:, :count, :]
        edge_ac = own_edges[:, count:, :]
        weight = own_flags[:count] * own_flags[count:]
        wanted = jnp.stack([second_local, vertex_point])
        asked = swapped(wanted, "tile", level_bit)
        picked, picked_flags = pick_pairs(visibility, flag_values, asked[0], asked[1])
        edge_bc, flag_bc = swapped((picked, picked_flags.astype(jnp.bfloat16)), "tile", level_bit)
        weight = weight * flag_bc.astype(jnp.float32)
        real_part, imag_part = bispectrum(edge_ab, edge_bc, edge_ac)
        weighted_real = weight[:, None] * real_part
        weighted_imag = weight[:, None] * imag_part
        magnitude = weight[:, None] * jnp.sqrt(real_part * real_part + imag_part * imag_part)
        spec_real = spec_real + jnp.sum(weighted_real, 0)
        spec_imag = spec_imag + jnp.sum(weighted_imag, 0)
        spec_norm = spec_norm + jnp.sum(magnitude, 0)
        channel_sums = jnp.stack([jnp.sum(weighted_real, 1), jnp.sum(weighted_imag, 1)])
        level_sums[level_bit] = channel_sums
    joined = jnp.concatenate(level_sums, axis=1)
    joined = taken_together(joined, "grp")
    triangle_means = joined / RADIO_BANDS
    spec_real, spec_imag, spec_norm = (
        sum_at_owner(spec_real, "tile", 0),
        sum_at_owner(spec_imag, "tile", 0),
        sum_at_owner(spec_norm, "tile", 0),
    )
    closure_spectrum = jnp.stack([spec_real, spec_imag]) / (1.0 + spec_norm)
    return (triangle_means, closure_spectrum)


def solution(mesh):
    placed = (P(None, "tile", None, "grp"), P("tile", None), P(None, "tile"))
    return jax.shard_map(
        body,
        mesh=mesh,
        in_specs=placed,
        out_specs=(P(None, "tile"), P(None, ("grp", "tile"))),
        check_vma=False,
    )
```

profile of v0, /device:TPU:1, one launch (start us, length us, event | category | flops | bytes accessed | tf_op | source)
XLA Modules:
  0.0 170.3 jit_solution(2051909488829143656)
XLA Ops:
  0.6 0.9 broadcast_subtract_fusion.1
  1.6 2.2 %collective-permute-start.3 = (s32[2,1024]{1,0:T(2,128)S(1)}, s32[2,1024]{1,0:T(2,128)S(1)}, u32[]{:S(2)}, u32[]{:S(2)}) collective-permute-start(s32[2,1024]{1,0:T(2,128)S(1)} %pad_add_fusion.1), channel_id=1, source_target_pairs={{0,2},{1,3},{2,0},{3,1},{4,6},{5,7},{6,4},{7,5},{8,10},{9,11},{10,... | collective-permute-start | bytes 24584 | tf_op jit(solution)/shard_map/ppermute | solution.py:12
  3.8 1.2 collective-permute-start
  5.0 0.8 convert_bitcast_fusion
  5.8 13.1 %gather_fusion.4 = bf16[2048]{0:T(1024)(128)(2,1)S(1)} fusion(bf16[8192]{0:T(1024)(128)(2,1)S(1)} %bitcast.77, s32[2048]{0:T(1024)S(1)} %broadcast_clamp_fusion), kind=kCustom, calls=%fused_computation.4.clone | custom fusion | bytes 16384 | tf_op jit(solution)/shard_map/jit(_take)/gather | solution.py:58
  18.9 13.1 %gather_fusion = bf16[2048]{0:T(1024)(128)(2,1)S(1)} fusion(bf16[8192]{0:T(1024)(128)(2,1)S(1)} %bitcast.78, s32[2048]{0:T(1024)S(1)} %broadcast_clamp_fusion.1), kind=kCustom, calls=%fused_computation.clone | custom fusion | bytes 16384 | tf_op jit(solution)/shard_map/jit(_take)/gather | solution.py:58
  31.9 8.4 %copy.67 = bf16[2,16,512,128]{3,0,2,1:T(2,128)(2,1)} copy(bf16[2,16,512,128]{3,2,1,0:T(8,128)(2,1)} %param.11) | data formatting | bytes 8388608 | tf_op args[0]
  40.4 9.2 %gather_fusion.6 = bf16[2048,2,128]{2,1,0:T(2,128)(2,1)S(1)} fusion(bf16[2,8192,128]{2,0,1:T(2,128)(2,1)} %bitcast.81, s32[2048]{0:T(1024)S(1)} %broadcast_clamp_fusion), kind=kCustom, calls=%fused_computation.6.clone | custom fusion | bytes 2105344 | tf_op jit(solution)/shard_map/jit(_take)/gather | solution.py:57
  49.6 9.2 %gather_fusion.2 = bf16[2048,2,128]{2,1,0:T(2,128)(2,1)S(1)} fusion(bf16[2,8192,128]{2,0,1:T(2,128)(2,1)} %bitcast.82, s32[2048]{0:T(1024)S(1)} %broadcast_clamp_fusion.1), kind=kCustom, calls=%fused_computation.2.clone | custom fusion | bytes 2105344 | tf_op jit(solution)/shard_map/jit(_take)/gather | solution.py:57
  58.9 0.7 fusion
  59.6 1.1 slice_convert_fusion.1
  60.7 0.6 fusion.1
  61.4 0.1 slice_convert_fusion.3
  61.5 0.0 collective-permute-done.3
  61.5 6.8 %gather_fusion.5 = bf16[1024]{0:T(1024)(128)(2,1)S(1)} fusion(bf16[8192]{0:T(1024)(128)(2,1)S(1)} %bitcast.79, s32[1024]{0:T(1024)S(1)} %fusion.25), kind=kCustom, calls=%fused_computation.5.clone | custom fusion | bytes 8192 | tf_op jit(solution)/shard_map/jit(_take)/gather | solution.py:58
  68.4 9.3 %gather_fusion.7 = bf16[1024,2,128]{2,1,0:T(2,128)(2,1)} fusion(bf16[2,8192,128]{2,0,1:T(2,128)(2,1)} %bitcast.83, s32[1024]{0:T(1024)S(1)} %fusion.25), kind=kCustom, calls=%fused_computation.7.clone | custom fusion | bytes 1052672 | tf_op jit(solution)/shard_map/jit(_take)/gather | solution.py:57
  77.7 0.0 collective-permute-done
  77.7 6.8 %gather_fusion.1 = bf16[1024]{0:T(1024)(128)(2,1)S(1)} fusion(bf16[8192]{0:T(1024)(128)(2,1)S(1)} %bitcast.80, s32[1024]{0:T(1024)S(1)} %fusion.24), kind=kCustom, calls=%fused_computation.1.clone | custom fusion | bytes 8192 | tf_op jit(solution)/shard_map/jit(_take)/gather | solution.py:58
  84.5 9.3 %gather_fusion.3 = bf16[1024,2,128]{2,1,0:T(2,128)(2,1)} fusion(bf16[2,8192,128]{2,0,1:T(2,128)(2,1)} %bitcast.84, s32[1024]{0:T(1024)S(1)} %fusion.24), kind=kCustom, calls=%fused_computation.3.clone | custom fusion | bytes 1052672 | tf_op jit(solution)/shard_map/jit(_take)/gather | solution.py:57
  93.8 0.0 copy-start
  93.8 1.8 %collective-permute-start.4 = (bf16[1024]{0:T(1024)(128)(2,1)S(1)}, bf16[1024]{0:T(1024)(128)(2,1)S(1)}, u32[]{:S(2)}, u32[]{:S(2)}) collective-permute-start(bf16[1024]{0:T(1024)(128)(2,1)S(1)} %get-tuple-element.23), channel_id=1, source_target_pairs={{0,2},{1,3},{2,0},{3,1},{4,6},{5,7},{6,4},{7,5},{8,10},{9,11},{10,... | collective-permute-start | bytes 6152 | tf_op jit(solution)/shard_map/ppermute | solution.py:12
  95.6 0.3 collective-permute-start.1
  95.9 1.2 fusion.10
  97.2 0.1 collective-permute-start.5
  97.3 1.2 fusion.11
  98.5 0.8 collective-permute-start.2
  99.4 0.0 collective-permute-done.4
  99.4 0.0 collective-permute-done.1
  99.4 11.1 %collective-permute-done.5 = bf16[2,1024,128]{2,1,0:T(8,128)(2,1)S(1)} collective-permute-done((bf16[2,1024,128]{2,1,0:T(8,128)(2,1)S(1)}, bf16[2,1024,128]{2,1,0:T(8,128)(2,1)S(1)}, u32[]{:S(2)}, u32[]{:S(2)}) %collective-permute-start.5) | collective-permute-done | bytes 524320 | tf_op jit(solution)/shard_map/ppermute | solution.py:12
  110.6 0.1 convert_element_type.46
  110.6 0.0 copy-done
  110.6 0.2 multiply_add_fusion
  110.9 0.0 collective-permute-done.2
  110.9 0.1 convert_element_type.41
  111.0 0.2 multiply_add_fusion.2
  111.2 0.6 fusion.5
  111.8 0.6 fusion.9
  112.4 0.7 add.130
  113.1 8.0 %all-to-all-start.1 = ((f32[32,1,4]{2,1,0:T(1,128)}), f32[32,1,4]{2,1,0:T(1,128)S(1)}, u32[]{:S(2)}, u32[]{:S(2)}) async-start(f32[32,1,4]{2,1,0:T(1,128)} %bitcast.21), calls=%async_computation.1 | async-start | bytes 32768 | tf_op jit(solution)/shard_map/all_to_all | solution.py:35
  121.2 0.7 add.136
  121.9 6.6 %all-to-all-done.1 = f32[32,1,4]{2,1,0:T(1,128)S(1)} async-done(((f32[32,1,4]{2,1,0:T(1,128)}), f32[32,1,4]{2,1,0:T(1,128)S(1)}, u32[]{:S(2)}, u32[]{:S(2)}) %all-to-all-start.1) | async-done | bytes 544 | tf_op jit(solution)/shard_map/all_to_all | solution.py:35
  128.4 4.1 %all-to-all-start.3 = ((f32[32,1,4]{2,1,0:T(1,128)}), f32[32,1,4]{2,1,0:T(1,128)S(1)}, u32[]{:S(2)}, u32[]{:S(2)}) async-start(f32[32,1,4]{2,1,0:T(1,128)} %bitcast.25), calls=%async_computation.3 | async-start | bytes 32768 | tf_op jit(solution)/shard_map/all_to_all | solution.py:35
  132.6 0.7 add.132
  133.3 6.7 %all-to-all-done.3 = f32[32,1,4]{2,1,0:T(1,128)S(1)} async-done(((f32[32,1,4]{2,1,0:T(1,128)}), f32[32,1,4]{2,1,0:T(1,128)S(1)}, u32[]{:S(2)}, u32[]{:S(2)}) %all-to-all-start.3) | async-done | bytes 544 | tf_op jit(solution)/shard_map/all_to_all | solution.py:35
  140.0 4.1 %all-to-all-start.2 = ((f32[32,1,4]{2,1,0:T(1,128)}), f32[32,1,4]{2,1,0:T(1,128)S(1)}, u32[]{:S(2)}, u32[]{:S(2)}) async-start(f32[32,1,4]{2,1,0:T(1,128)} %bitcast.23), calls=%async_computation.2 | async-start | bytes 32768 | tf_op jit(solution)/shard_map/all_to_all | solution.py:35
  144.2 0.1 reduce_sum.139
  144.2 7.3 %all-to-all-done.2 = f32[32,1,4]{2,1,0:T(1,128)S(1)} async-done(((f32[32,1,4]{2,1,0:T(1,128)}), f32[32,1,4]{2,1,0:T(1,128)S(1)}, u32[]{:S(2)}, u32[]{:S(2)}) %all-to-all-start.2) | async-done | bytes 544 | tf_op jit(solution)/shard_map/all_to_all | solution.py:35
  151.5 0.7 broadcast_in_dim.43
  152.2 7.9 %all-to-all-start = ((f32[8,2,2048]{2,1,0:T(2,128)}), f32[8,2,2048]{2,1,0:T(2,128)S(1)}, u32[]{:S(2)}, u32[]{:S(2)}) async-start(f32[8,2,2048]{2,1,0:T(2,128)} %broadcast_in_dim.43), calls=%async_computation | async-start | bytes 262144 | tf_op jit(solution)/shard_map/all_to_all | solution.py:17
  160.2 0.1 reduce_sum.133
  160.2 0.1 reduce_sum.136
  160.3 0.6 maximum_divide_fusion
  160.8 8.8 %all-to-all-done = f32[8,2,2048]{2,1,0:T(2,128)S(1)} async-done(((f32[8,2,2048]{2,1,0:T(2,128)}), f32[8,2,2048]{2,1,0:T(2,128)S(1)}, u32[]{:S(2)}, u32[]{:S(2)}) %all-to-all-start) | async-done | bytes 131104 | tf_op jit(solution)/shard_map/all_to_all | solution.py:17
  169.7 0.6 broadcast_multiply_fusion
  (21 shorter events, 0.2 us)
Async XLA Ops:
  1.6 59.9 %collective-permute-start.3 = (s32[2,1024]{1,0:T(2,128)S(1)}, s32[2,1024]{1,0:T(2,128)S(1)}, u32[]{:S(2)}, u32[]{:S(2)}) collective-permute-start(s32[2,1024]{1,0:T(2,128)S(1)} %pad_add_fusion.1), channel_id=1, source_target_pairs={{0,2},{1,3},{2,0},{3,1},{4,6},{5,7},{6,4},{7,5},{8,10},{9,11},{10,... | collective-permute-start | bytes 24584 | tf_op jit(solution)/shard_map/ppermute | solution.py:12
  3.8 73.9 %collective-permute-start = (s32[2,1024]{1,0:T(2,128)S(1)}, s32[2,1024]{1,0:T(2,128)S(1)}, u32[]{:S(2)}, u32[]{:S(2)}) collective-permute-start(s32[2,1024]{1,0:T(2,128)S(1)} %pad_add_fusion), channel_id=1, source_target_pairs={{0,1},{1,0},{2,3},{3,2},{4,5},{5,4},{6,7},{7,6},{8,9},{9,8},{10,11... | collective-permute-start | bytes 24584 | tf_op jit(solution)/shard_map/ppermute | solution.py:12
  93.8 16.8 %copy-start = (f32[2,1024,128]{2,1,0:T(8,128)S(1)}, f32[2,1024,128]{2,1,0:T(8,128)}, u32[]{:S(2)}) copy-start(f32[2,1024,128]{2,1,0:T(8,128)} %get-tuple-element.32) | copy-start | bytes 3145732
  93.8 5.6 %collective-permute-start.4 = (bf16[1024]{0:T(1024)(128)(2,1)S(1)}, bf16[1024]{0:T(1024)(128)(2,1)S(1)}, u32[]{:S(2)}, u32[]{:S(2)}) collective-permute-start(bf16[1024]{0:T(1024)(128)(2,1)S(1)} %get-tuple-element.23), channel_id=1, source_target_pairs={{0,2},{1,3},{2,0},{3,1},{4,6},{5,7},{6,4},{7,5},{8,10},{9,11},{10,... | collective-permute-start | bytes 6152 | tf_op jit(solution)/shard_map/ppermute | solution.py:12
  95.6 3.8 %collective-permute-start.1 = (bf16[1024]{0:T(1024)(128)(2,1)S(1)}, bf16[1024]{0:T(1024)(128)(2,1)S(1)}, u32[]{:S(2)}, u32[]{:S(2)}) collective-permute-start(bf16[1024]{0:T(1024)(128)(2,1)S(1)} %get-tuple-element.16), channel_id=1, source_target_pairs={{0,1},{1,0},{2,3},{3,2},{4,5},{5,4},{6,7},{7,6},{8,9},{9,8},{10,11... | collective-permute-start | bytes 6152 | tf_op jit(solution)/shard_map/ppermute | solution.py:12
  97.2 13.4 %collective-permute-start.5 = (bf16[2,1024,128]{2,1,0:T(8,128)(2,1)S(1)}, bf16[2,1024,128]{2,1,0:T(8,128)(2,1)S(1)}, u32[]{:S(2)}, u32[]{:S(2)}) collective-permute-start(bf16[2,1024,128]{2,1,0:T(8,128)(2,1)S(1)} %fusion.10), channel_id=1, source_target_pairs={{0,2},{1,3},{2,0},{3,1},{4,6},{5,7},{6,4},{7,5},{8,10},{9,11},{10,... | collective-permute-start | bytes 1572872 | tf_op jit(solution)/shard_map/ppermute | solution.py:12
  98.5 12.3 %collective-permute-start.2 = (bf16[2,1024,128]{2,1,0:T(8,128)(2,1)S(1)}, bf16[2,1024,128]{2,1,0:T(8,128)(2,1)S(1)}, u32[]{:S(2)}, u32[]{:S(2)}) collective-permute-start(bf16[2,1024,128]{2,1,0:T(8,128)(2,1)S(1)} %fusion.11), channel_id=1, source_target_pairs={{0,1},{1,0},{2,3},{3,2},{4,5},{5,4},{6,7},{7,6},{8,9},{9,8},{10,11... | collective-permute-start | bytes 1572872 | tf_op jit(solution)/shard_map/ppermute | solution.py:12
  113.1 15.3 %all-to-all-start.1 = ((f32[32,1,4]{2,1,0:T(1,128)}), f32[32,1,4]{2,1,0:T(1,128)S(1)}, u32[]{:S(2)}, u32[]{:S(2)}) async-start(f32[32,1,4]{2,1,0:T(1,128)} %bitcast.21), calls=%async_computation.1 | async-start | bytes 32768 | tf_op jit(solution)/shard_map/all_to_all | solution.py:35
  128.4 11.6 %all-to-all-start.3 = ((f32[32,1,4]{2,1,0:T(1,128)}), f32[32,1,4]{2,1,0:T(1,128)S(1)}, u32[]{:S(2)}, u32[]{:S(2)}) async-start(f32[32,1,4]{2,1,0:T(1,128)} %bitcast.25), calls=%async_computation.3 | async-start | bytes 32768 | tf_op jit(solution)/shard_map/all_to_all | solution.py:35
  140.0 11.5 %all-to-all-start.2 = ((f32[32,1,4]{2,1,0:T(1,128)}), f32[32,1,4]{2,1,0:T(1,128)S(1)}, u32[]{:S(2)}, u32[]{:S(2)}) async-start(f32[32,1,4]{2,1,0:T(1,128)} %bitcast.23), calls=%async_computation.2 | async-start | bytes 32768 | tf_op jit(solution)/shard_map/all_to_all | solution.py:35
  152.2 17.4 %all-to-all-start = ((f32[8,2,2048]{2,1,0:T(2,128)}), f32[8,2,2048]{2,1,0:T(2,128)S(1)}, u32[]{:S(2)}, u32[]{:S(2)}) async-start(f32[8,2,2048]{2,1,0:T(2,128)} %broadcast_in_dim.43), calls=%async_computation | async-start | bytes 262144 | tf_op jit(solution)/shard_map/all_to_all | solution.py:17
where the time goes:
time: 171 us; the launch traced here: 170 us
  local copies, waits for them, and re-layouts  88.1 us (52%)
  waiting for transfers between devices  40.5 us (24%)
  starting transfers between devices  30.7 us (18%)
  other arithmetic  10.1 us (6%)
    gather x4, local copies, waits for them, and re-layouts, pick_pairs(): flags = jnp.take(flag_flat, flat_index, axis=0).astype(jnp.float32)  39.8 us
    gather x4, local copies, waits for them, and re-layouts, pick_pairs(): edges = jnp.take(planes, flat_index, axis=1)  37.1 us
    all_to_all x3, waiting for transfers between devices, sum_at_owner(): lax.all_to_all(parts, axis, split_axis=0, concat_axis=0, tiled=True)  20.6 us
    all_to_all x3, starting transfers between devices, sum_at_owner(): lax.all_to_all(parts, axis, split_axis=0, concat_axis=0, tiled=True)  16.3 us
    ppermute x6, waiting for transfers between devices, swapped(): lax.ppermute(array, axis, [(i, i ^ 1 << stride) for i in range(lax.axis_s...  11.2 us
    all_to_all x1, waiting for transfers between devices, copy_for_each(): lax.all_to_all(jnp.broadcast_to(array[None], (devices, *array.shape)), ax...  8.76 us
    unnamed x4, local copies, waits for them, and re-layouts  8.46 us
    all_to_all x1, starting transfers between devices, copy_for_each(): lax.all_to_all(jnp.broadcast_to(array[None], (devices, *array.shape)), ax...  7.95 us
  transfers between devices with their start and end apart: 10, of which 5 were waited for; matrix products, arithmetic and copies ran while one was open for 46% of the time, Pallas kernels for 0%

commit v1 on v0

v1 whole, which is shorter than its diff:
```python
import jax
import jax.numpy as jnp
from jax import lax
from jax.experimental import pallas as pl
from jax.experimental.pallas import tpu as pltpu
from jax.sharding import PartitionSpec as P

RADIO_BANDS = 1024
TRI_LVL = 1024
LEVELS = 2
CHUNK = 256
CHUNKS = TRI_LVL // CHUNK
PIECES = LEVELS * CHUNKS
UNROLL = 32
MESH = pl.DeviceIdType.MESH
GROUPS = ((0, 4), (4, 3), (7, 1))


def kernel(
    vis_hbm, okay_hbm, tri_hbm, means_ref, closure_ref,
    vis, okay, tri, mask, table, ask, asked, own_pq, own_pr,
    s_asked, s_pq, s_pr,
    edge_a, edge_b, product, give, got, split, part, arrived, spec, spec_in,
    load_sem, vis_sem, smem_sem, ask_send, ask_recv, row_send, row_recv,
    mean_send, mean_recv, spec_send, spec_recv,
):
    tile = lax.axis_index("tile")
    grp = lax.axis_index("grp")
    tiles = lax.axis_size("tile")
    grps = lax.axis_size("grp")
    block = vis.shape[1]
    dishes = vis.shape[2]
    quarter = block // 4

    load_tri = pltpu.make_async_copy(tri_hbm, tri, load_sem.at[0])
    load_tri.start()
    load_okay = pltpu.make_async_copy(okay_hbm, okay, load_sem.at[1])
    load_okay.start()
    loads = []
    for k in range(4):
        rows = pl.ds(k * quarter, quarter)
        load = pltpu.make_async_copy(vis_hbm.at[:, rows], vis.at[:, rows], vis_sem.at[k])
        load.start()
        loads.append(load)

    barrier = pltpu.get_barrier_semaphore()
    for k in range(1, tiles):
        pl.semaphore_signal(barrier, inc=1, device_id={"tile": lax.rem(tile + k, tiles)}, device_id_type=MESH)
    for k in range(1, grps):
        pl.semaphore_signal(barrier, inc=1, device_id={"grp": lax.rem(grp + k, grps)}, device_id_type=MESH)

    partner = [tile + 1 - 2 * lax.rem(tile, 2), tile + 2 - 4 * lax.rem(lax.div(tile, 2), 2)]

    load_tri.wait()
    for lvl in range(LEVELS):
        cols = pl.ds(lvl * TRI_LVL, TRI_LVL)
        first = jnp.bitwise_and(tri[0:1, cols], block - 1)
        second = tri[1:2, cols]
        third = tri[2:3, cols]
        own_pq[:, cols] = first * dishes + second
        own_pr[:, cols] = first * dishes + third
        ask[lvl] = jnp.bitwise_and(second, block - 1) * dishes + third
    to_pq = pltpu.make_async_copy(own_pq, s_pq, smem_sem.at[0])
    to_pq.start()
    to_pr = pltpu.make_async_copy(own_pr, s_pr, smem_sem.at[1])
    to_pr.start()

    pl.semaphore_wait(barrier, tiles - 1 + grps - 1)
    asks = []
    for lvl in (1, 0):
        send = pltpu.make_async_remote_copy(
            src_ref=ask.at[lvl], dst_ref=asked.at[lvl],
            send_sem=ask_send.at[lvl], recv_sem=ask_recv.at[lvl],
            device_id={"tile": partner[lvl]}, device_id_type=MESH,
        )
        send.start()
        asks.append(send)

    load_okay.wait()
    flags_t = jnp.transpose(okay[...].astype(jnp.float32)).astype(jnp.bfloat16)

    rows_of = table.reshape(2 * block * dishes, table.shape[2])

    def build_row(p, _):
        pick = (lax.broadcasted_iota(jnp.int32, (block, 128), 0) == p).astype(jnp.float32).astype(jnp.bfloat16)
        mask[...] = jnp.dot(flags_t, pick, preferred_element_type=jnp.float32)

        def build(i, _):
            for u in range(4):
                r = pl.multiple_of((i * 4 + u) * 16, 16)
                keep = mask[pl.ds(r, 16), :]
                base = p * (2 * dishes) + 2 * r
                rows_of[pl.ds(base, 16, stride=2), :] = vis[0, p, pl.ds(r, 16), :].astype(jnp.float32) * keep
                rows_of[pl.ds(base + 1, 16, stride=2), :] = vis[1, p, pl.ds(r, 16), :].astype(jnp.float32) * keep
            return 0

        lax.fori_loop(0, dishes // 64, build, 0)
        return 0

    for k in range(4):
        loads[k].wait()
        lax.fori_loop(k * quarter, (k + 1) * quarter, build_row, 0)
    to_pq.wait()
    to_pr.wait()

    def gather(index, start, dst):
        def body(g, _):
            for u in range(UNROLL):
                j = g * UNROLL + u
                dst[pl.ds(pl.multiple_of(2 * j, 2), 2), :] = table[index(start + j)]
            return 0

        lax.fori_loop(0, CHUNK // UNROLL, body, 0)

    def own(piece):
        gather(lambda j: s_pq[0, j], piece * CHUNK, edge_a)
        gather(lambda j: s_pr[0, j], piece * CHUNK, edge_b)

        def body(g, _):
            r = pl.multiple_of(g * 32, 32)
            a_re = edge_a[pl.ds(r, 16, stride=2), :]
            a_im = edge_a[pl.ds(r + 1, 16, stride=2), :]
            b_re = edge_b[pl.ds(r, 16, stride=2), :]
            b_im = edge_b[pl.ds(r + 1, 16, stride=2), :]
            at = pl.ds(pl.multiple_of(g * 16, 16), 16)
            product[piece, 0, at, :] = a_re * b_re + a_im * b_im
            product[piece, 1, at, :] = a_im * b_re - a_re * b_im
            return 0

        lax.fori_loop(0, CHUNK // 16, body, 0)

    def serve(lvl, chunk):
        piece = lvl * CHUNKS + chunk
        gather(lambda j: s_asked[lvl, 0, j], chunk * CHUNK, edge_a)

        def body(g, _):
            r = pl.multiple_of(g * 32, 32)
            at = pl.ds(pl.multiple_of(g * 16, 16), 16)
            give[piece, 0, at, :] = edge_a[pl.ds(r, 16, stride=2), :].astype(jnp.bfloat16)
            give[piece, 1, at, :] = edge_a[pl.ds(r + 1, 16, stride=2), :].astype(jnp.bfloat16)
            return 0

        lax.fori_loop(0, CHUNK // 16, body, 0)
        send = pltpu.make_async_remote_copy(
            src_ref=give.at[piece], dst_ref=got.at[piece],
            send_sem=row_send.at[piece], recv_sem=row_recv.at[piece],
            device_id={"tile": partner[lvl]}, device_id_type=MESH,
        )
        send.start()
        return send

    ones = jnp.ones((8, 128), jnp.bfloat16)

    def combine(piece, sums):
        def body(g, sums):
            at = pl.ds(pl.multiple_of(g * 16, 16), 16)
            p_re = product[piece, 0, at, :]
            p_im = product[piece, 1, at, :]
            c_re = got[piece, 0, at, :].astype(jnp.float32)
            c_im = got[piece, 1, at, :].astype(jnp.float32)
            re = p_re * c_re - p_im * c_im
            im = p_re * c_im + p_im * c_re
            mag = jnp.sqrt(re * re + im * im)
            re_hi = re.astype(jnp.bfloat16)
            im_hi = im.astype(jnp.bfloat16)
            split[0, at, :] = re_hi
            split[1, at, :] = (re - re_hi.astype(jnp.float32)).astype(jnp.bfloat16)
            split[2, at, :] = im_hi
            split[3, at, :] = (im - im_hi.astype(jnp.float32)).astype(jnp.bfloat16)
            return (
                sums[0] + re[:8] + re[8:],
                sums[1] + im[:8] + im[8:],
                sums[2] + mag[:8] + mag[8:],
            )

        sums = lax.fori_loop(0, CHUNK // 16, body, sums)

        def lanes(k):
            return lax.dot_general(ones, split[k], (((1,), (1,)), ((), ())), preferred_element_type=jnp.float32)

        part[piece, 0:1, :] = (lanes(0) + lanes(1))[0:1]
        part[piece, 1:2, :] = (lanes(2) + lanes(3))[0:1]
        arrived[0, piece] = part[piece]
        return sums

    def share(n):
        start, count = GROUPS[n]
        sends = []
        for k in range(1, grps):
            send = pltpu.make_async_remote_copy(
                src_ref=part.at[pl.ds(start, count)], dst_ref=arrived.at[k, pl.ds(start, count)],
                send_sem=mean_send.at[n, k - 1], recv_sem=mean_recv.at[n, k - 1],
                device_id={"grp": lax.rem(grp + k, grps)}, device_id_type=MESH,
            )
            send.start()
            sends.append(send)
        return sends

    def index_in(lvl):
        asks[1 - lvl].wait_recv()
        copy = pltpu.make_async_copy(asked.at[lvl], s_asked.at[lvl], smem_sem.at[2 + lvl])
        copy.start()
        return copy

    index_in(1).wait()
    sends = [serve(1, c) for c in range(CHUNKS)]
    index_in(0).wait()
    sends0 = [serve(0, c) for c in range(CHUNKS)]
    zero = jnp.zeros((8, 128), jnp.float32)
    sums = (zero, zero, zero)
    for c in range(CHUNKS):
        own(c)
    for c in range(CHUNKS):
        sends0[c].wait_recv()
        sums = combine(c, sums)
    mean_sends = share(0)
    for c in range(CHUNKS):
        own(CHUNKS + c)
    for c in range(CHUNKS):
        sends[c].wait_recv()
        sums = combine(CHUNKS + c, sums)
        if c == CHUNKS - 2:
            mean_sends += share(1)
    mean_sends += share(2)

    for k in range(3):
        spec[k : k + 1, :] = jnp.sum(sums[k], axis=0, keepdims=True)
    spec[3:4, :] = jnp.zeros((1, 128), jnp.float32)
    spec_in[0] = spec[...]
    spec_sends = []
    for k in range(1, tiles):
        send = pltpu.make_async_remote_copy(
            src_ref=spec, dst_ref=spec_in.at[k],
            send_sem=spec_send.at[k - 1], recv_sem=spec_recv.at[k - 1],
            device_id={"tile": lax.rem(tile + k, tiles)}, device_id_type=MESH,
        )
        send.start()
        spec_sends.append(send)

    def finish(n):
        start, count = GROUPS[n]
        for send in mean_sends[n * (grps - 1) : (n + 1) * (grps - 1)]:
            send.wait_recv()
        total = arrived[lax.rem(grp + grps, grps), pl.ds(start, count)]
        for s in range(1, grps):
            total = total + arrived[lax.rem(grp - s + grps, grps), pl.ds(start, count)]
        total = total * (1.0 / RADIO_BANDS)
        for c in range(count):
            means_ref[:, pl.ds((start + c) * CHUNK, CHUNK)] = total[c]

    for n in range(len(GROUPS)):
        finish(n)
    for send in spec_sends:
        send.wait_recv()
    total = jnp.sum(spec_in[...], axis=0)
    closure_ref[...] = total[0:2] / (1.0 + total[2:3])

    for send in asks + sends + sends0 + mean_sends + spec_sends:
        send.wait_send()


def fused(visibility, dish_pair_okay, triangles):
    block, dishes, channels = visibility.shape[1:]
    tiles = lax.axis_size("tile")
    grps = lax.axis_size("grp")
    f32, bf16, i32 = jnp.float32, jnp.bfloat16, jnp.int32
    groups = len(GROUPS)
    dma = pltpu.SemaphoreType.DMA
    return pl.pallas_call(
        kernel,
        out_shape=(
            jax.ShapeDtypeStruct((2, LEVELS * TRI_LVL), f32),
            jax.ShapeDtypeStruct((2, channels), f32),
        ),
        in_specs=[pl.BlockSpec(memory_space=pl.ANY)] * 3,
        out_specs=(pl.BlockSpec(memory_space=pltpu.VMEM), pl.BlockSpec(memory_space=pltpu.VMEM)),
        scratch_shapes=[
            pltpu.VMEM((2, block, dishes, channels), bf16),
            pltpu.VMEM((block, dishes), i32),
            pltpu.VMEM((3, LEVELS * TRI_LVL), i32),
            pltpu.VMEM((dishes, channels), f32),
            pltpu.VMEM((block * dishes, 2, channels), f32),
            pltpu.VMEM((LEVELS, 1, TRI_LVL), i32),
            pltpu.VMEM((LEVELS, 1, TRI_LVL), i32),
            pltpu.VMEM((1, LEVELS * TRI_LVL), i32),
            pltpu.VMEM((1, LEVELS * TRI_LVL), i32),
            pltpu.SMEM((LEVELS, 1, TRI_LVL), i32),
            pltpu.SMEM((1, LEVELS * TRI_LVL), i32),
            pltpu.SMEM((1, LEVELS * TRI_LVL), i32),
            pltpu.VMEM((2 * CHUNK, channels), f32),
            pltpu.VMEM((2 * CHUNK, channels), f32),
            pltpu.VMEM((PIECES, 2, CHUNK, channels), f32),
            pltpu.VMEM((PIECES, 2, CHUNK, channels), bf16),
            pltpu.VMEM((PIECES, 2, CHUNK, channels), bf16),
            pltpu.VMEM((4, CHUNK, channels), bf16),
            pltpu.VMEM((PIECES, 2, CHUNK), f32),
            pltpu.VMEM((grps, PIECES, 2, CHUNK), f32),
            pltpu.VMEM((4, channels), f32),
            pltpu.VMEM((tiles, 4, channels), f32),
            dma((2,)), dma((4,)), dma((4,)),
            dma((LEVELS,)), dma((LEVELS,)),
            dma((PIECES,)), dma((PIECES,)),
            dma((groups, grps - 1)), dma((groups, grps - 1)),
            dma((tiles - 1,)), dma((tiles - 1,)),
        ],
        compiler_params=pltpu.CompilerParams(collective_id=0, has_side_effects=True, vmem_limit_bytes=48 * 2**20),
        name="closure",
    )(visibility, dish_pair_okay, triangles)


def body(visibility, dish_pair_okay, triangles):
    means, closure = fused(visibility, dish_pair_okay, triangles)
    tile = lax.axis_index("tile")
    width = closure.shape[1] // lax.axis_size("tile")
    return means, lax.dynamic_slice(closure, (0, tile * width), (2, width))


def solution(mesh):
    placed = (P(None, "tile", None, "grp"), P("tile", None), P(None, "tile"))
    return jax.shard_map(
        body,
        mesh=mesh,
        in_specs=placed,
        out_specs=(P(None, "tile"), P(None, ("grp", "tile"))),
        check_vma=False,
    )
```

time: 171 us -> 44.7 us (0.26)
  local copies, waits for them, and re-layouts: 88.1 us -> 4.94 us
  waiting for transfers between devices: 40.5 us -> 0 us
  Pallas kernels: 0 us -> 38.9 us
  starting transfers between devices: 30.7 us -> 0 us
  other arithmetic: 10.1 us -> 0 us
    gather x8 -> x0, local copies, waits for them, and re-layouts: 76.8 us -> none  [the longest x4 39.8 us: pick_pairs(): flags = jnp.take(flag_flat, flat_index, axis=0).astype(jnp.float32)]
    pallas_call x0 -> x1, Pallas kernels: none -> 38.9 us  [fused(): pl.pallas_call(kernel, out_shape=(jax.ShapeDtypeStruct((2, LEVELS * TRI_L...]
    all_to_all x4 -> x0, waiting for transfers between devices: 29.3 us -> none  [the longest x3 20.6 us: sum_at_owner(): lax.all_to_all(parts, axis, split_axis=0, concat_axis=0, tiled=True)]
    all_to_all x4 -> x0, starting transfers between devices: 24.2 us -> none  [the longest x3 16.3 us: sum_at_owner(): lax.all_to_all(parts, axis, split_axis=0, concat_axis=0, tiled=True)]
    ppermute x6 -> x0, waiting for transfers between devices: 11.2 us -> none  [swapped(): lax.ppermute(array, axis, [(i, i ^ 1 << stride) for i in range(lax.axis_s...]
    ppermute x6 -> x0, starting transfers between devices: 6.45 us -> none  [swapped(): lax.ppermute(array, axis, [(i, i ^ 1 << stride) for i in range(lax.axis_s...]
    unnamed x4 -> x7, local copies, waits for them, and re-layouts: 8.46 us -> 4.3 us
    select_n x6 -> x0, other arithmetic: 3.81 us -> none  [the longest x4 3.79 us: pick_pairs(): edges = jnp.take(planes, flat_index, axis=1)]
  transfers between devices with their start and end apart: 10 -> 0, of which waited for: 5 -> 0; matrix products, arithmetic and copies ran while one was open for 46% -> 0% of each run, Pallas kernels for 0% -> 0%
where the time goes in v1:
time: 44.7 us; the launch traced here: 44.5 us
  Pallas kernels  38.9 us (87%)
  local copies, waits for them, and re-layouts  4.94 us (11%)
  between operations  0.65 us (1%)
    pallas_call x1, Pallas kernels, fused(): pl.pallas_call(kernel, out_shape=(jax.ShapeDtypeStruct((2, LEVELS * TRI_L...  38.9 us
    unnamed x7, local copies, waits for them, and re-layouts  4.3 us

profile of v1, /device:TPU:1, one launch (start us, length us, event | category | flops | bytes accessed | tf_op | source)
XLA Modules:
  0.0 44.5 jit_solution(5505603713985273681)
XLA Ops:
  0.6 0.0 copy-start
  0.6 2.2 %copy-done = bf16[2,16,512,128]{3,2,1,0:T(8,128)(2,1)S(1)} copy-done((bf16[2,16,512,128]{3,2,1,0:T(8,128)(2,1)S(1)}, bf16[2,16,512,128]{3,2,1,0:T(8,128)(2,1)}, u32[]{:S(2)}) %copy-start) | copy-done | bytes 4194328
  2.8 0.0 copy-start.1
  2.8 0.8 %copy-done.1 = s32[16,512]{1,0:T(8,128)S(1)} copy-done((s32[16,512]{1,0:T(8,128)S(1)}, s32[16,512]{1,0:T(8,128)}, u32[]{:S(2)}) %copy-start.1) | copy-done | bytes 32792
  3.6 0.0 copy-start.2
  3.6 0.8 %copy-done.2 = s32[3,2048]{1,0:T(4,128)S(1)} copy-done((s32[3,2048]{1,0:T(4,128)S(1)}, s32[3,2048]{1,0:T(4,128)}, u32[]{:S(2)}) %copy-start.2) | copy-done | bytes 24600
  4.3 38.9 %closure.1 = (f32[2,2048]{1,0:T(2,128)S(1)}, f32[2,128]{1,0:T(2,128)S(1)}) custom-call(bf16[2,16,512,128]{3,2,1,0:T(8,128)(2,1)S(1)} %copy-done, s32[16,512]{1,0:T(8,128)S(1)} %copy-done.1, s32[3,2048]{1,0:T(4,128)S(1)} %copy-done.2), custom_call_target="tpu_custom_call" | custom-call | tf_op jit(solution)/shard_map/closure/pallas_call | solution.py:269
  43.2 0.6 %constant_dynamic-slice_fusion = f32[2,4]{1,0:T(2,128)} fusion(f32[2,128]{1,0:T(2,128)S(1)} %get-tuple-element.5, s32[]{:T(128)S(6)} %select_n.3), kind=kLoop, calls=%fused_computation | loop fusion | bytes 68 | tf_op jit(solution)/shard_map/dynamic_slice | solution.py:315
  43.8 0.6 %copy.6 = f32[2,2048]{1,0:T(2,128)} copy(f32[2,2048]{1,0:T(2,128)S(1)} %get-tuple-element.8) | data formatting | bytes 32768
Async XLA Ops:
  0.6 2.2 %copy-start = (bf16[2,16,512,128]{3,2,1,0:T(8,128)(2,1)S(1)}, bf16[2,16,512,128]{3,2,1,0:T(8,128)(2,1)}, u32[]{:S(2)}) copy-start(bf16[2,16,512,128]{3,2,1,0:T(8,128)(2,1)} %vis_hbm.1) | copy-start | bytes 12582916
  2.8 0.8 %copy-start.1 = (s32[16,512]{1,0:T(8,128)S(1)}, s32[16,512]{1,0:T(8,128)}, u32[]{:S(2)}) copy-start(s32[16,512]{1,0:T(8,128)} %okay_hbm.1) | copy-start | bytes 98308
  3.6 0.8 %copy-start.2 = (s32[3,2048]{1,0:T(4,128)S(1)}, s32[3,2048]{1,0:T(4,128)}, u32[]{:S(2)}) copy-start(s32[3,2048]{1,0:T(4,128)} %tri_hbm.1) | copy-start | bytes 73732

commit v2 on v1

--- a/solution.py
+++ b/solution.py
@@ -8,20 +8,23 @@
 RADIO_BANDS = 1024
 TRI_LVL = 1024
 LEVELS = 2
-CHUNK = 256
+CHUNK = 128
 CHUNKS = TRI_LVL // CHUNK
 PIECES = LEVELS * CHUNKS
 UNROLL = 32
 MESH = pl.DeviceIdType.MESH
-GROUPS = ((0, 4), (4, 3), (7, 1))
+NEAR = ((1, 0, 0, 0), (-1, 0, 0, 0), (0, 1, 0, 0), (0, -1, 0, 0), (0, 0, 1, 0), (0, 0, -1, 0), (0, 0, 0, 1))
+SECOND = ((0, 0, 0, 1), (2, 0, 0, 0), (0, 2, 0, 0), (0, 0, 2, 0), (0, 0, -2, 0))
+THIRD = ((0, 0, 2, 0), (0, 0, -2, 0))
+GROUPS = ((0, 8), (8, 7), (15, 1))
 
 
 def kernel(
     vis_hbm, okay_hbm, tri_hbm, means_ref, closure_ref,
     vis, okay, tri, mask, table, ask, asked, own_pq, own_pr,
-    s_asked, s_pq, s_pr,
+    s_asked0, s_asked1, s_pq, s_pr,
     edge_a, edge_b, product, give, got, split, part, arrived, spec, spec_in,
-    load_sem, vis_sem, smem_sem, ask_send, ask_recv, row_send, row_recv,
+    known, load_sem, vis_sem, smem_sem, ask_send, ask_recv, row_send, row_recv,
     mean_send, mean_recv, spec_send, spec_recv,
 ):
     tile = lax.axis_index("tile")
@@ -44,10 +47,16 @@
         loads.append(load)
 
     barrier = pltpu.get_barrier_semaphore()
-    for k in range(1, tiles):
-        pl.semaphore_signal(barrier, inc=1, device_id={"tile": lax.rem(tile + k, tiles)}, device_id_type=MESH)
-    for k in range(1, grps):
-        pl.semaphore_signal(barrier, inc=1, device_id={"grp": lax.rem(grp + k, grps)}, device_id_type=MESH)
+    spots = (lax.rem(grp, 4), lax.rem(lax.div(tile, 2), 4), lax.div(grp, 4) * 4 + lax.div(tile, 8), lax.rem(tile, 2))
+
+    def tell(sem, steps):
+        for step in steps:
+            x, y, z, core = (lax.rem(at + d + n, n) for at, d, n in zip(spots, step, (4, 4, 8, 2)))
+            there = {"grp": lax.div(z, 4) * 4 + x, "tile": lax.rem(z, 4) * 8 + y * 2 + core}
+            pl.semaphore_signal(sem, inc=1, device_id=there, device_id_type=MESH)
+
+    tell(barrier, NEAR)
+    s_asked = (s_asked0, s_asked1)
 
     partner = [tile + 1 - 2 * lax.rem(tile, 2), tile + 2 - 4 * lax.rem(lax.div(tile, 2), 2)]
 
@@ -65,7 +74,8 @@
     to_pr = pltpu.make_async_copy(own_pr, s_pr, smem_sem.at[1])
     to_pr.start()
 
-    pl.semaphore_wait(barrier, tiles - 1 + grps - 1)
+    pl.semaphore_wait(barrier, len(NEAR))
+    tell(known.at[0], NEAR)
     asks = []
     for lvl in (1, 0):
         send = pltpu.make_async_remote_copy(
@@ -131,7 +141,7 @@
 
     def serve(lvl, chunk):
         piece = lvl * CHUNKS + chunk
-        gather(lambda j: s_asked[lvl, 0, j], chunk * CHUNK, edge_a)
+        gather(lambda j: s_asked[lvl][0, j], chunk * CHUNK, edge_a)
 
         def body(g, _):
             r = pl.multiple_of(g * 32, 32)
@@ -198,14 +208,18 @@
 
     def index_in(lvl):
         asks[1 - lvl].wait_recv()
-        copy = pltpu.make_async_copy(asked.at[lvl], s_asked.at[lvl], smem_sem.at[2 + lvl])
+        copy = pltpu.make_async_copy(asked.at[lvl], s_asked[lvl], smem_sem.at[2 + lvl])
         copy.start()
         return copy
 
     index_in(1).wait()
     sends = [serve(1, c) for c in range(CHUNKS)]
+    pl.semaphore_wait(known.at[0], len(NEAR))
+    tell(known.at[1], SECOND)
     index_in(0).wait()
     sends0 = [serve(0, c) for c in range(CHUNKS)]
+    pl.semaphore_wait(known.at[1], len(SECOND))
+    tell(known.at[2], THIRD)
     zero = jnp.zeros((8, 128), jnp.float32)
     sums = (zero, zero, zero)
     for c in range(CHUNKS):
@@ -213,6 +227,7 @@
     for c in range(CHUNKS):
         sends0[c].wait_recv()
         sums = combine(c, sums)
+    pl.semaphore_wait(known.at[2], len(THIRD))
     mean_sends = share(0)
     for c in range(CHUNKS):
         own(CHUNKS + c)
@@ -272,7 +287,7 @@
             jax.ShapeDtypeStruct((2, LEVELS * TRI_LVL), f32),
             jax.ShapeDtypeStruct((2, channels), f32),
         ),
-        in_specs=[pl.BlockSpec(memory_space=pl.ANY)] * 3,
+        in_specs=[pl.BlockSpec(memory_space=pltpu.HBM)] * 3,
         out_specs=(pl.BlockSpec(memory_space=pltpu.VMEM), pl.BlockSpec(memory_space=pltpu.VMEM)),
         scratch_shapes=[
             pltpu.VMEM((2, block, dishes, channels), bf16),
@@ -284,7 +299,8 @@
             pltpu.VMEM((LEVELS, 1, TRI_LVL), i32),
             pltpu.VMEM((1, LEVELS * TRI_LVL), i32),
             pltpu.VMEM((1, LEVELS * TRI_LVL), i32),
-            pltpu.SMEM((LEVELS, 1, TRI_LVL), i32),
+            pltpu.SMEM((1, TRI_LVL), i32),
+            pltpu.SMEM((1, TRI_LVL), i32),
             pltpu.SMEM((1, LEVELS * TRI_LVL), i32),
             pltpu.SMEM((1, LEVELS * TRI_LVL), i32),
             pltpu.VMEM((2 * CHUNK, channels), f32),
@@ -297,13 +313,14 @@
             pltpu.VMEM((grps, PIECES, 2, CHUNK), f32),
             pltpu.VMEM((4, channels), f32),
             pltpu.VMEM((tiles, 4, channels), f32),
+            pltpu.SemaphoreType.REGULAR((3,)),
             dma((2,)), dma((4,)), dma((4,)),
             dma((LEVELS,)), dma((LEVELS,)),
             dma((PIECES,)), dma((PIECES,)),
             dma((groups, grps - 1)), dma((groups, grps - 1)),
             dma((tiles - 1,)), dma((tiles - 1,)),
         ],
-        compiler_params=pltpu.CompilerParams(collective_id=0, has_side_effects=True, vmem_limit_bytes=48 * 2**20),
+        compiler_params=pltpu.CompilerParams(collective_id=0, has_side_effects=True, vmem_limit_bytes=67043328),
         name="closure",
     )(visibility, dish_pair_okay, triangles)
 

time: 44.7 us -> 39.8 us (0.89)
  Pallas kernels: 38.9 us -> 36.4 us
  local copies, waits for them, and re-layouts: 4.94 us -> 2.62 us
    unnamed x7 -> x1, local copies, waits for them, and re-layouts: 4.3 us -> 1.32 us
    pallas_call x1, Pallas kernels: 38.9 us -> 36.4 us  [fused(): pl.pallas_call(kernel, out_shape=(jax.ShapeDtypeStruct((2, LEVELS * TRI_L...]
    dynamic_slice x1, local copies, waits for them, and re-layouts: 0.64 us -> 1.29 us  [body(): return (means, lax.dynamic_slice(closure, (0, tile * width), (2, width)))]
where the time goes in v2:
time: 39.8 us; the launch traced here: 39.6 us
  Pallas kernels  36.4 us (91%)
  local copies, waits for them, and re-layouts  2.62 us (7%)
  between operations  0.64 us (2%)
    pallas_call x1, Pallas kernels, fused(): pl.pallas_call(kernel, out_shape=(jax.ShapeDtypeStruct((2, LEVELS * TRI_L...  36.4 us
    unnamed x1, local copies, waits for them, and re-layouts  1.32 us
    dynamic_slice x1, local copies, waits for them, and re-layouts, body(): return (means, lax.dynamic_slice(closure, (0, tile * width), (2, width)))  1.29 us

profile of v2, /device:TPU:1, one launch (start us, length us, event | category | flops | bytes accessed | tf_op | source)
XLA Modules:
  0.0 39.6 jit_solution(16559973807906754813)
XLA Ops:
  0.6 36.4 %closure.1 = (f32[2,2048]{1,0:T(2,128)}, f32[2,128]{1,0:T(2,128)}) custom-call(bf16[2,16,512,128]{3,2,1,0:T(8,128)(2,1)} %vis_hbm.1, s32[16,512]{1,0:T(8,128)} %okay_hbm.1, s32[3,2048]{1,0:T(4,128)} %tri_hbm.1), custom_call_target="tpu_custom_call" | custom-call | tf_op jit(solution)/shard_map/closure/pallas_call | solution.py:284
  37.0 1.3 %constant_dynamic-slice_fusion = f32[2,4]{1,0:T(2,128)} fusion(f32[2,128]{1,0:T(2,128)} %get-tuple-element.5, s32[]{:T(128)S(6)} %select_n.3), kind=kLoop, calls=%fused_computation | loop fusion | bytes 68 | tf_op jit(solution)/shard_map/dynamic_slice | solution.py:332
  38.3 1.3 %copy.6 = f32[2,2048]{1,0:T(2,128)} copy(f32[2,2048]{1,0:T(2,128)} %get-tuple-element.8) | data formatting | bytes 32768

commit v3 on v2

v3 whole, which is shorter than its diff:
```python
import jax
import jax.numpy as jnp
from jax import lax
from jax.experimental import pallas as pl
from jax.experimental.pallas import tpu as pltpu
from jax.sharding import PartitionSpec as P

RADIO_BANDS = 1024
TRI_LVL = 1024
LEVELS = 2
CHUNK = 128
CHUNKS = TRI_LVL // CHUNK
PIECES = LEVELS * CHUNKS
UNROLL = 32
EARLY_ROWS = 12
MESH = pl.DeviceIdType.MESH
NEAR = ((1, 0, 0, 0), (-1, 0, 0, 0), (0, 1, 0, 0), (0, -1, 0, 0), (0, 0, 1, 0), (0, 0, -1, 0), (0, 0, 0, 1))
SECOND = ((0, 0, 0, 1), (2, 0, 0, 0), (0, 2, 0, 0), (0, 0, 2, 0), (0, 0, -2, 0))
THIRD = ((0, 0, 2, 0), (0, 0, -2, 0))
GROUPS = ((0, 8), (8, 4), (12, 2), (14, 1), (15, 1))


def kernel(
    vis_hbm, okay_hbm, tri_hbm, means_ref, closure_ref,
    vis, okay, tri, mask, table, ask, asked, own_pr, s_asked0, s_asked1, s_pr,
    edge_ab, edge_bc, edge_ac, product, give, got, split, spec, spec_in, part, arrived,
    known, load_sem, vis_sem, smem_sem, ask_send, ask_recv, row_send, row_recv,
    mean_send, mean_recv, spec_send, spec_recv,
):
    f32, bf16 = jnp.float32, jnp.bfloat16
    tile = lax.axis_index("tile")
    grp = lax.axis_index("grp")
    tiles = lax.axis_size("tile")
    grps = lax.axis_size("grp")
    block, dishes, channels = vis.shape[1:]
    s_asked = (s_asked0, s_asked1)

    load_tri = pltpu.make_async_copy(tri_hbm, tri, load_sem.at[0])
    load_tri.start()
    load_okay = pltpu.make_async_copy(okay_hbm, okay, load_sem.at[1])
    load_okay.start()

    def load_row(p):
        return pltpu.make_async_copy(vis_hbm.at[:, p], vis.at[:, p], vis_sem.at[p])

    for p in range(block):
        load_row(p).start()

    barrier = pltpu.get_barrier_semaphore()
    spots = (lax.rem(grp, 4), lax.rem(lax.div(tile, 2), 4), lax.div(grp, 4) * 4 + lax.div(tile, 8), lax.rem(tile, 2))

    def tell(sem, steps):
        for step in steps:
            x, y, z, core = (lax.rem(at + d + n, n) for at, d, n in zip(spots, step, (4, 4, 8, 2)))
            there = {"grp": lax.div(z, 4) * 4 + x, "tile": lax.rem(z, 4) * 8 + y * 2 + core}
            pl.semaphore_signal(sem, inc=1, device_id=there, device_id_type=MESH)

    tell(barrier, NEAR)
    partner = [tile + 1 - 2 * lax.rem(tile, 2), tile + 2 - 4 * lax.rem(lax.div(tile, 2), 2)]

    with jax.named_scope("tri_wait"):
        load_tri.wait()
    first = jnp.bitwise_and(tri[0:1, :], block - 1)
    second = jnp.bitwise_and(tri[1:2, :], block - 1)
    third = tri[2:3, :]
    wanted = second * dishes + third
    for lvl in range(LEVELS):
        ask[lvl] = wanted[:, lvl * TRI_LVL : (lvl + 1) * TRI_LVL]

    with jax.named_scope("barrier"):
        pl.semaphore_wait(barrier, len(NEAR))
    tell(known.at[0], NEAR)
    asks = []
    for lvl in range(LEVELS):
        asks.append(
            pltpu.make_async_remote_copy(
                src_ref=ask.at[lvl], dst_ref=asked.at[lvl],
                send_sem=ask_send.at[lvl], recv_sem=ask_recv.at[lvl],
                device_id={"tile": partner[lvl]}, device_id_type=MESH,
            )
        )
    asks[1].start()
    asks[0].start()
    own_pr[...] = first * dishes + third
    to_pr = pltpu.make_async_copy(own_pr, s_pr, smem_sem.at[2])
    to_pr.start()
    pair = (first * block + second).astype(f32)

    with jax.named_scope("flags"):
        load_okay.wait()
        flags_t = jnp.transpose(okay[...].astype(f32)).astype(bf16)
        for c in range(0, block, 2):
            row = lax.broadcasted_iota(jnp.int32, (block, 2 * channels), 0)
            col = lax.broadcasted_iota(jnp.int32, (block, 2 * channels), 1)
            pick = jnp.where(row == c + (col >= channels).astype(jnp.int32), 1.0, 0.0).astype(bf16)
            both = jnp.dot(flags_t, pick, preferred_element_type=f32).astype(bf16)
            mask[c] = both[:, :channels]
            mask[c + 1] = both[:, channels:]

    flat = table.reshape(2 * block * dishes, channels)

    def build(p, _):
        load_row(p).wait()
        for r in range(0, dishes, 16):
            keep = mask[p, r : r + 16, :]
            base = p * (2 * dishes) + 2 * r
            flat[pl.ds(base, 16, stride=2), :] = (vis[0, p, r : r + 16, :] * keep).astype(f32)
            flat[pl.ds(base + 1, 16, stride=2), :] = (vis[1, p, r : r + 16, :] * keep).astype(f32)
        return 0

    with jax.named_scope("build"):
        lax.fori_loop(0, EARLY_ROWS, build, 0)
    to_asked = []
    with jax.named_scope("ask_wait"):
        for lvl in (1, 0):
            asks[lvl].wait_recv()
            copy = pltpu.make_async_copy(asked.at[lvl], s_asked[lvl], smem_sem.at[lvl])
            copy.start()
            to_asked.append(copy)
    with jax.named_scope("build_late"):
        lax.fori_loop(EARLY_ROWS, block, build, 0)

    def gather(index, start, dst):
        def body(g, _):
            for u in range(UNROLL):
                j = g * UNROLL + u
                dst[pl.ds(pl.multiple_of(2 * j, 2), 2), :] = table[index[0, start + j]]
            return 0

        lax.fori_loop(0, CHUNK // UNROLL, body, 0)

    def serve(lvl, chunk):
        piece = lvl * CHUNKS + chunk
        gather(s_asked[lvl], chunk * CHUNK, edge_bc)
        for r in range(0, CHUNK, 16):
            give[piece, 0, r : r + 16, :] = edge_bc[pl.ds(2 * r, 16, stride=2), :].astype(bf16)
            give[piece, 1, r : r + 16, :] = edge_bc[pl.ds(2 * r + 1, 16, stride=2), :].astype(bf16)
        send = pltpu.make_async_remote_copy(
            src_ref=give.at[piece], dst_ref=got.at[piece],
            send_sem=row_send.at[piece], recv_sem=row_recv.at[piece],
            device_id={"tile": partner[lvl]}, device_id_type=MESH,
        )
        send.start()
        return send

    def own(lvl):
        start = pl.multiple_of(partner[lvl] * block, block)
        for p in range(block):
            keep = mask[p, pl.ds(start, block), :]
            at = slice(p * block, (p + 1) * block)
            edge_ab[at, :channels] = vis[0, p, pl.ds(start, block), :] * keep
            edge_ab[at, channels:] = vis[1, p, pl.ds(start, block), :] * keep
        codes = [pair[:, (lvl * CHUNKS + c) * CHUNK : (lvl * CHUNKS + c + 1) * CHUNK] for c in range(CHUNKS)]
        codes_t = jnp.transpose(jnp.concatenate(codes, axis=0))
        lane = lax.broadcasted_iota(jnp.int32, (CHUNK, block * block), 1).astype(f32)
        for c in range(CHUNKS):
            piece = lvl * CHUNKS + c
            hot = jnp.where(lane == codes_t[:, c : c + 1], 1.0, 0.0).astype(bf16)
            ab = jnp.dot(hot, edge_ab[...], preferred_element_type=f32)
            gather(s_pr, piece * CHUNK, edge_ac)
            for r in range(0, CHUNK, 16):
                a_re = ab[r : r + 16, :channels]
                a_im = ab[r : r + 16, channels:]
                b_re = edge_ac[pl.ds(2 * r, 16, stride=2), :]
                b_im = edge_ac[pl.ds(2 * r + 1, 16, stride=2), :]
                product[piece, 0, r : r + 16, :] = a_re * b_re + a_im * b_im
                product[piece, 1, r : r + 16, :] = a_im * b_re - a_re * b_im

    def combine(piece, row, sums, total):
        slot = piece % 2

        def body(g, sums):
            at = pl.ds(pl.multiple_of(g * 16, 16), 16)
            low = pl.ds(pl.multiple_of(CHUNK + g * 16, 16), 16)
            p_re = product[piece, 0, at, :]
            p_im = product[piece, 1, at, :]
            c_re = got[piece, 0, at, :].astype(f32)
            c_im = got[piece, 1, at, :].astype(f32)
            re = p_re * c_re - p_im * c_im
            im = p_re * c_im + p_im * c_re
            mag = jnp.sqrt(re * re + im * im)
            re_hi = re.astype(bf16)
            im_hi = im.astype(bf16)
            split[slot, at, :channels] = re_hi
            split[slot, at, channels:] = (re - re_hi.astype(f32)).astype(bf16)
            split[slot, low, :channels] = im_hi
            split[slot, low, channels:] = (im - im_hi.astype(f32)).astype(bf16)
            return (
                sums[0] + (re[:8] + re[8:]),
                sums[1] + (im[:8] + im[8:]),
                sums[2] + (mag[:8] + mag[8:]),
            )

        sums = lax.fori_loop(0, CHUNK // 16, body, sums)
        ones = jnp.where(lax.broadcasted_iota(jnp.int32, (8, 2 * channels), 0) == row, 1.0, 0.0).astype(bf16)
        lanes = lax.dot_general(ones, split[slot], (((1,), (1,)), ((), ())), preferred_element_type=f32)
        return sums, lanes if total is None else total + lanes

    def share(n, total):
        count = GROUPS[n][1]
        part[n][...] = total[:count]
        arrived[n][0] = total[:count]
        sends = []
        for k in range(1, grps):
            send = pltpu.make_async_remote_copy(
                src_ref=part[n], dst_ref=arrived[n].at[k],
                send_sem=mean_send.at[n, k - 1], recv_sem=mean_recv.at[n, k - 1],
                device_id={"grp": lax.rem(grp + k, grps)}, device_id_type=MESH,
            )
            send.start()
            sends.append(send)
        return sends

    for copy in to_asked[:1]:
        copy.wait()
    rows = [None] * LEVELS
    with jax.named_scope("serve1"):
        rows[1] = [serve(1, c) for c in range(CHUNKS)]
    with jax.named_scope("known0"):
        pl.semaphore_wait(known.at[0], len(NEAR))
    tell(known.at[1], SECOND)
    to_asked[1].wait()
    with jax.named_scope("serve0"):
        rows[0] = [serve(0, c) for c in range(CHUNKS)]
    to_pr.wait()
    zero = jnp.zeros((8, channels), f32)
    sums = (zero, zero, zero)
    mean_sends = []
    for lvl in range(LEVELS):
        with jax.named_scope(f"own{lvl}"):
            own(lvl)
        if lvl == 0:
            with jax.named_scope("known1"):
                pl.semaphore_wait(known.at[1], len(SECOND))
            tell(known.at[2], THIRD)
        for n, (start, count) in enumerate(GROUPS):
            if start // CHUNKS != lvl:
                continue
            total = None
            for k in range(count):
                piece = start + k
                with jax.named_scope(f"rows{lvl}"):
                    rows[lvl][piece % CHUNKS].wait_recv()
                with jax.named_scope(f"combine{lvl}"):
                    sums, total = combine(piece, k, sums, total)
            if n == 0:
                with jax.named_scope("known2"):
                    pl.semaphore_wait(known.at[2], len(THIRD))
            with jax.named_scope("share"):
                mean_sends.append(share(n, total))

    with jax.named_scope("spec_send"):
        for k in range(3):
            spec[k : k + 1, :] = jnp.sum(sums[k], axis=0, keepdims=True)
        spec[3:4, :] = jnp.zeros((1, channels), f32)
        spec_in[0] = spec[...]
        spec_sends = []
        for k in range(1, tiles):
            send = pltpu.make_async_remote_copy(
                src_ref=spec, dst_ref=spec_in.at[k],
                send_sem=spec_send.at[k - 1], recv_sem=spec_recv.at[k - 1],
                device_id={"tile": lax.rem(tile + k, tiles)}, device_id_type=MESH,
            )
            send.start()
            spec_sends.append(send)

    for n, (start, count) in enumerate(GROUPS):
        with jax.named_scope(f"finish{n}"):
            for send in mean_sends[n]:
                send.wait_recv()
            total = arrived[n][grp]
            for s in range(1, grps):
                total = total + arrived[n][lax.rem(grp - s + grps, grps)]
            total = total * (1.0 / RADIO_BANDS)
            for k in range(count):
                at = slice((start + k) * CHUNK, (start + k + 1) * CHUNK)
                means_ref[0:1, at] = total[k : k + 1, :CHUNK]
                means_ref[1:2, at] = total[k : k + 1, CHUNK:]

    with jax.named_scope("spec_wait"):
        for send in spec_sends:
            send.wait_recv()
        total = jnp.sum(spec_in[...], axis=0)
        closure_ref[...] = total[0:2] / (1.0 + total[2:3])

    with jax.named_scope("send_wait"):
        for send in asks + rows[0] + rows[1] + sum(mean_sends, []) + spec_sends:
            send.wait_send()


def fused(visibility, dish_pair_okay, triangles):
    block, dishes, channels = visibility.shape[1:]
    tiles = lax.axis_size("tile")
    grps = lax.axis_size("grp")
    f32, bf16, i32 = jnp.float32, jnp.bfloat16, jnp.int32
    groups = len(GROUPS)
    dma = pltpu.SemaphoreType.DMA
    return pl.pallas_call(
        kernel,
        out_shape=(
            jax.ShapeDtypeStruct((2, LEVELS * TRI_LVL), f32),
            jax.ShapeDtypeStruct((2, channels), f32),
        ),
        in_specs=[pl.BlockSpec(memory_space=pltpu.HBM)] * 3,
        out_specs=(pl.BlockSpec(memory_space=pltpu.VMEM), pl.BlockSpec(memory_space=pltpu.VMEM)),
        scratch_shapes=[
            pltpu.VMEM((2, block, dishes, channels), bf16),
            pltpu.VMEM((block, dishes), i32),
            pltpu.VMEM((3, LEVELS * TRI_LVL), i32),
            pltpu.VMEM((block, dishes, channels), bf16),
            pltpu.VMEM((block * dishes, 2, channels), f32),
            pltpu.VMEM((LEVELS, 1, TRI_LVL), i32),
            pltpu.VMEM((LEVELS, 1, TRI_LVL), i32),
            pltpu.VMEM((1, LEVELS * TRI_LVL), i32),
            pltpu.SMEM((1, TRI_LVL), i32),
            pltpu.SMEM((1, TRI_LVL), i32),
            pltpu.SMEM((1, LEVELS * TRI_LVL), i32),
            pltpu.VMEM((block * block, 2 * channels), bf16),
            pltpu.VMEM((2 * CHUNK, channels), f32),
            pltpu.VMEM((2 * CHUNK, channels), f32),
            pltpu.VMEM((PIECES, 2, CHUNK, channels), f32),
            pltpu.VMEM((PIECES, 2, CHUNK, channels), bf16),
            pltpu.VMEM((PIECES, 2, CHUNK, channels), bf16),
            pltpu.VMEM((2, 2 * CHUNK, 2 * channels), bf16),
            pltpu.VMEM((4, channels), f32),
            pltpu.VMEM((tiles, 4, channels), f32),
            [pltpu.VMEM((count, 2 * CHUNK), f32) for _, count in GROUPS],
            [pltpu.VMEM((grps, count, 2 * CHUNK), f32) for _, count in GROUPS],
            pltpu.SemaphoreType.REGULAR((3,)),
            dma((2,)), dma((block,)), dma((3,)),
            dma((LEVELS,)), dma((LEVELS,)),
            dma((PIECES,)), dma((PIECES,)),
            dma((groups, grps - 1)), dma((groups, grps - 1)),
            dma((tiles - 1,)), dma((tiles - 1,)),
        ],
        compiler_params=pltpu.CompilerParams(
            collective_id=0, has_side_effects=True, vmem_limit_bytes=67043328 - 24 * 1024
        ),
        name="closure",
    )(visibility, dish_pair_okay, triangles)


def body(visibility, dish_pair_okay, triangles):
    means, closure = fused(visibility, dish_pair_okay, triangles)
    tile = lax.axis_index("tile")
    width = closure.shape[1] // lax.axis_size("tile")
    return means, lax.dynamic_slice(closure, (0, tile * width), (2, width))


def solution(mesh):
    placed = (P(None, "tile", None, "grp"), P("tile", None), P(None, "tile"))
    return jax.shard_map(
        body,
        mesh=mesh,
        in_specs=placed,
        out_specs=(P(None, "tile"), P(None, ("grp", "tile"))),
        check_vma=False,
    )
```

time: 39.8 us -> 36.8 us (0.925)
  Pallas kernels: 36.4 us -> 33.4 us
    pallas_call x1, Pallas kernels: 36.4 us -> 33.4 us  [fused(): pl.pallas_call(kernel, out_shape=(jax.ShapeDtypeStruct((2, LEVELS * TRI_L...]
where the time goes in v3:
time: 36.8 us; the launch traced here: 36.6 us
  Pallas kernels  33.4 us (91%)
  local copies, waits for them, and re-layouts  2.62 us (7%)
  between operations  0.64 us (2%)
    pallas_call x1, Pallas kernels, fused(): pl.pallas_call(kernel, out_shape=(jax.ShapeDtypeStruct((2, LEVELS * TRI_L...  33.4 us
    unnamed x1, local copies, waits for them, and re-layouts  1.32 us
    dynamic_slice x1, local copies, waits for them, and re-layouts, body(): return (means, lax.dynamic_slice(closure, (0, tile * width), (2, width)))  1.29 us

profile of v3, /device:TPU:1, one launch (start us, length us, event | category | flops | bytes accessed | tf_op | source)
XLA Modules:
  0.0 36.6 jit_solution(6050045296418803985)
XLA Ops:
  0.6 33.4 %closure.1 = (f32[2,2048]{1,0:T(2,128)}, f32[2,128]{1,0:T(2,128)}) custom-call(bf16[2,16,512,128]{3,2,1,0:T(8,128)(2,1)} %vis_hbm.1, s32[16,512]{1,0:T(8,128)} %okay_hbm.1, s32[3,2048]{1,0:T(4,128)} %tri_hbm.1), custom_call_target="tpu_custom_call" | custom-call | tf_op jit(solution)/shard_map/closure/pallas_call | solution.py:298
  34.0 1.3 %constant_dynamic-slice_fusion = f32[2,4]{1,0:T(2,128)} fusion(f32[2,128]{1,0:T(2,128)} %get-tuple-element.5, s32[]{:T(128)S(6)} %select_n.3), kind=kLoop, calls=%fused_computation | loop fusion | bytes 68 | tf_op jit(solution)/shard_map/dynamic_slice | solution.py:347
  35.3 1.3 %copy.6 = f32[2,2048]{1,0:T(2,128)} copy(f32[2,2048]{1,0:T(2,128)} %get-tuple-element.8) | data formatting | bytes 32768

commit v4 on v3

v4 whole, which is shorter than its diff:
```python
import jax
import jax.numpy as jnp
from jax import lax
from jax.experimental import pallas as pl
from jax.experimental.pallas import tpu as pltpu
from jax.sharding import PartitionSpec as P

RADIO_BANDS = 1024
TRI_LVL = 1024
LEVELS = 2
CHUNK = 128
CHUNKS = TRI_LVL // CHUNK
PIECES = LEVELS * CHUNKS
UNROLL = 32
ROWS = 4
MESH = pl.DeviceIdType.MESH
NEAR = ((1, 0, 0, 0), (-1, 0, 0, 0), (0, 1, 0, 0), (0, -1, 0, 0), (0, 0, 1, 0), (0, 0, -1, 0), (0, 0, 0, 1))
SECOND = ((0, 0, 0, 1), (2, 0, 0, 0), (0, 2, 0, 0), (0, 0, 2, 0), (0, 0, -2, 0))
THIRD = ((0, 0, 2, 0), (0, 0, -2, 0))
GROUPS = ((0, 8), (8, 4), (12, 2), (14, 1), (15, 1))


def kernel(
    vis_hbm, okay_hbm, tri_hbm, means_ref, closure_ref,
    vis, okay, tri, mask, table, ask, own_pr, s_asked0, s_asked1, s_pr,
    pairs, edge_ab, edge_bc, edge_ac, give, got, split, spec, spec_in, part, arrived,
    known, load_sem, vis_sem, smem_sem, ask_send, ask_recv, row_send, row_recv,
    mean_send, mean_recv, spec_send, spec_recv,
):
    f32, bf16 = jnp.float32, jnp.bfloat16
    tile = lax.axis_index("tile")
    grp = lax.axis_index("grp")
    tiles = lax.axis_size("tile")
    grps = lax.axis_size("grp")
    block, dishes, channels = vis.shape[1:]
    s_asked = (s_asked0, s_asked1)

    load_tri = pltpu.make_async_copy(tri_hbm, tri, load_sem.at[0])
    load_tri.start()
    load_okay = pltpu.make_async_copy(okay_hbm, okay, load_sem.at[1])
    load_okay.start()

    def load_rows(k):
        rows = pl.ds(k * ROWS, ROWS)
        return pltpu.make_async_copy(vis_hbm.at[:, rows], vis.at[:, rows], vis_sem.at[k])

    barrier = pltpu.get_barrier_semaphore()
    spots = (lax.rem(grp, 4), lax.rem(lax.div(tile, 2), 4), lax.div(grp, 4) * 4 + lax.div(tile, 8), lax.rem(tile, 2))

    def tell(sem, steps):
        for step in steps:
            x, y, z, core = (lax.rem(at + d + n, n) for at, d, n in zip(spots, step, (4, 4, 8, 2)))
            there = {"grp": lax.div(z, 4) * 4 + x, "tile": lax.rem(z, 4) * 8 + y * 2 + core}
            pl.semaphore_signal(sem, inc=1, device_id=there, device_id_type=MESH)

    tell(barrier, NEAR)
    partner = [tile + 1 - 2 * lax.rem(tile, 2), tile + 2 - 4 * lax.rem(lax.div(tile, 2), 2)]

    with jax.named_scope("tri_wait"):
        load_tri.wait()
    for k in range(block // ROWS):
        load_rows(k).start()
    first = jnp.bitwise_and(tri[0:1, :], block - 1)
    second = jnp.bitwise_and(tri[1:2, :], block - 1)
    third = tri[2:3, :]
    wanted = second * dishes + third
    for lvl in range(LEVELS):
        ask[lvl] = wanted[:, lvl * TRI_LVL : (lvl + 1) * TRI_LVL]

    with jax.named_scope("barrier"):
        pl.semaphore_wait(barrier, len(NEAR))
    tell(known.at[0], NEAR)
    asks = []
    for lvl in range(LEVELS):
        asks.append(
            pltpu.make_async_remote_copy(
                src_ref=ask.at[lvl], dst_ref=s_asked[lvl],
                send_sem=ask_send.at[lvl], recv_sem=ask_recv.at[lvl],
                device_id={"tile": partner[lvl]}, device_id_type=MESH,
            )
        )
    asks[1].start()
    asks[0].start()
    own_pr[...] = first * dishes + third
    to_pr = pltpu.make_async_copy(own_pr, s_pr, smem_sem)
    to_pr.start()
    pair = (first * block + second).astype(f32)

    with jax.named_scope("flags"):
        load_okay.wait()
        flags_t = jnp.transpose(okay[...].astype(f32)).astype(bf16)
        for c in range(0, block, 2):
            row = lax.broadcasted_iota(jnp.int32, (block, 2 * channels), 0)
            col = lax.broadcasted_iota(jnp.int32, (block, 2 * channels), 1)
            pick = jnp.where(row == c + (col >= channels).astype(jnp.int32), 1.0, 0.0).astype(bf16)
            both = jnp.dot(flags_t, pick, preferred_element_type=f32).astype(bf16)
            mask[c] = both[:, :channels]
            mask[c + 1] = both[:, channels:]

    flat = table.reshape(2 * block * dishes, channels)

    def build(p, _):
        for r in range(0, dishes, 16):
            keep = mask[p, r : r + 16, :]
            base = p * (2 * dishes) + 2 * r
            flat[pl.ds(base, 16, stride=2), :] = (vis[0, p, r : r + 16, :] * keep).astype(f32)
            flat[pl.ds(base + 1, 16, stride=2), :] = (vis[1, p, r : r + 16, :] * keep).astype(f32)
        return 0

    with jax.named_scope("build"):
        for k in range(block // ROWS):
            load_rows(k).wait()
            lax.fori_loop(k * ROWS, (k + 1) * ROWS, build, 0)
    with jax.named_scope("ask_wait"):
        asks[1].wait_recv()

    def gather(index, start, count, dst):
        def body(g, _):
            for u in range(UNROLL):
                j = g * UNROLL + u
                dst[pl.ds(pl.multiple_of(2 * j, 2), 2), :] = table[index[0, start + j]]
            return 0

        lax.fori_loop(0, count // UNROLL, body, 0)

    def serve(lvl, chunk):
        piece = lvl * CHUNKS + chunk
        gather(s_asked[lvl], chunk * CHUNK, CHUNK, edge_bc)
        for r in range(0, CHUNK, 16):
            give[piece, 0, r : r + 16, :] = edge_bc[pl.ds(2 * r, 16, stride=2), :].astype(bf16)
            give[piece, 1, r : r + 16, :] = edge_bc[pl.ds(2 * r + 1, 16, stride=2), :].astype(bf16)
        send = pltpu.make_async_remote_copy(
            src_ref=give.at[piece], dst_ref=got.at[piece],
            send_sem=row_send.at[lvl], recv_sem=row_recv.at[chunk if lvl else CHUNKS],
            device_id={"tile": partner[lvl]}, device_id_type=MESH,
        )
        send.start()
        return send

    def own(lvl):
        start = pl.multiple_of(partner[lvl] * block, block)
        for p in range(block):
            keep = mask[p, pl.ds(start, block), :]
            at = slice(p * block, (p + 1) * block)
            pairs[at, :channels] = vis[0, p, pl.ds(start, block), :] * keep
            pairs[at, channels:] = vis[1, p, pl.ds(start, block), :] * keep
        codes = [pair[:, (lvl * CHUNKS + c) * CHUNK : (lvl * CHUNKS + c + 1) * CHUNK] for c in range(CHUNKS)]
        codes_t = jnp.transpose(jnp.concatenate(codes, axis=0))
        lane = lax.broadcasted_iota(jnp.int32, (CHUNK, block * block), 1).astype(f32)
        for c in range(CHUNKS):
            hot = jnp.where(lane == codes_t[:, c : c + 1], 1.0, 0.0).astype(bf16)
            edge_ab[lvl, c] = jnp.dot(hot, pairs[...], preferred_element_type=f32)
        gather(s_pr, lvl * TRI_LVL, TRI_LVL, edge_ac.at[lvl])

    def multiply(lvl, chunk, r, sums):
        at = pl.ds(pl.multiple_of(r, 16), 16)
        low = pl.ds(pl.multiple_of(CHUNK + r, 16), 16)
        base = pl.multiple_of(2 * (chunk * CHUNK + r), 32)
        a_re = edge_ab[lvl, chunk, at, :channels]
        a_im = edge_ab[lvl, chunk, at, channels:]
        b_re = edge_ac[lvl, pl.ds(base, 16, stride=2), :]
        b_im = edge_ac[lvl, pl.ds(base + 1, 16, stride=2), :]
        p_re = a_re * b_re + a_im * b_im
        p_im = a_im * b_re - a_re * b_im
        c_re = got[lvl * CHUNKS + chunk, 0, at, :].astype(f32)
        c_im = got[lvl * CHUNKS + chunk, 1, at, :].astype(f32)
        re = p_re * c_re - p_im * c_im
        im = p_re * c_im + p_im * c_re
        mag = jnp.sqrt(re * re + im * im)
        re_hi = re.astype(bf16)
        im_hi = im.astype(bf16)
        split[chunk, at, :channels] = re_hi
        split[chunk, at, channels:] = (re - re_hi.astype(f32)).astype(bf16)
        split[chunk, low, :channels] = im_hi
        split[chunk, low, channels:] = (im - im_hi.astype(f32)).astype(bf16)
        return (
            sums[0] + (re[:8] + re[8:]),
            sums[1] + (im[:8] + im[8:]),
            sums[2] + (mag[:8] + mag[8:]),
        )

    def lanes(chunk, row):
        ones = jnp.where(lax.broadcasted_iota(jnp.int32, (8, 2 * channels), 0) == row, 1.0, 0.0).astype(bf16)
        return lax.dot_general(ones, split[chunk], (((1,), (1,)), ((), ())), preferred_element_type=f32)

    def multiply_chunk(lvl, chunk, sums):
        def body(g, sums):
            for u in range(2):
                sums = multiply(lvl, chunk, g * 32 + u * 16, sums)
            return sums

        return lax.fori_loop(0, CHUNK // 32, body, sums)

    def wait_all(sem, ref):
        pltpu.make_async_copy(ref, ref, sem).wait()

    def share(n, total):
        count = GROUPS[n][1]
        part[n][...] = total[:count]
        arrived[n][0] = total[:count]
        for k in range(1, grps):
            send = pltpu.make_async_remote_copy(
                src_ref=part[n], dst_ref=arrived[n].at[k],
                send_sem=mean_send.at[n], recv_sem=mean_recv.at[n],
                device_id={"grp": lax.rem(grp + k, grps)}, device_id_type=MESH,
            )
            send.start()

    rows = [None] * LEVELS
    with jax.named_scope("serve1"):
        rows[1] = [serve(1, c) for c in range(CHUNKS)]
    with jax.named_scope("known0"):
        pl.semaphore_wait(known.at[0], len(NEAR))
    tell(known.at[1], SECOND)
    asks[0].wait_recv()
    with jax.named_scope("serve0"):
        rows[0] = [serve(0, c) for c in range(CHUNKS)]
    to_pr.wait()
    zero = jnp.zeros((8, channels), f32)
    sums = (zero, zero, zero)
    with jax.named_scope("own0"):
        own(0)
    with jax.named_scope("known1"):
        pl.semaphore_wait(known.at[1], len(SECOND))
    tell(known.at[2], THIRD)
    with jax.named_scope("rows0"):
        wait_all(row_recv.at[CHUNKS], got.at[pl.ds(0, CHUNKS)])
    with jax.named_scope("combine0"):
        sums = lax.fori_loop(0, CHUNKS, lambda c, sums: multiply_chunk(0, c, sums), sums)
        total = lanes(0, 0)
        for c in range(1, CHUNKS):
            total = total + lanes(c, c)
    with jax.named_scope("own1"):
        own(1)
    with jax.named_scope("known2"):
        pl.semaphore_wait(known.at[2], len(THIRD))
    with jax.named_scope("share"):
        share(0, total)
    for n, (start, count) in enumerate(GROUPS[1:], 1):
        total = None
        for k in range(count):
            c = start + k - CHUNKS
            with jax.named_scope("rows1"):
                rows[1][c].wait_recv()
            with jax.named_scope("combine1"):
                sums = multiply_chunk(1, c, sums)
                total = lanes(c, k) if k == 0 else total + lanes(c, k)
        with jax.named_scope("share"):
            share(n, total)

    with jax.named_scope("spec_send"):
        for k in range(3):
            spec[k : k + 1, :] = jnp.sum(sums[k], axis=0, keepdims=True)
        spec[3:4, :] = jnp.zeros((1, channels), f32)
        spec_in[0] = spec[...]
        for k in range(1, tiles):
            send = pltpu.make_async_remote_copy(
                src_ref=spec, dst_ref=spec_in.at[k],
                send_sem=spec_send, recv_sem=spec_recv,
                device_id={"tile": lax.rem(tile + k, tiles)}, device_id_type=MESH,
            )
            send.start()

    for n, (start, count) in enumerate(GROUPS):
        with jax.named_scope(f"finish{n}"):
            wait_all(mean_recv.at[n], arrived[n].at[pl.ds(1, grps - 1)])
            total = arrived[n][grp]
            for s in range(1, grps):
                total = total + arrived[n][lax.rem(grp - s + grps, grps)]
            total = total * (1.0 / RADIO_BANDS)
            for k in range(count):
                at = slice((start + k) * CHUNK, (start + k + 1) * CHUNK)
                means_ref[0:1, at] = total[k : k + 1, :CHUNK]
                means_ref[1:2, at] = total[k : k + 1, CHUNK:]

    with jax.named_scope("spec_wait"):
        wait_all(spec_recv, spec_in.at[pl.ds(1, tiles - 1)])
        total = jnp.sum(spec_in[...], axis=0)
        closure_ref[...] = total[0:2] / (1.0 + total[2:3])

    with jax.named_scope("send_wait"):
        for lvl in range(LEVELS):
            asks[lvl].wait_send()
            wait_all(row_send.at[lvl], give.at[pl.ds(lvl * CHUNKS, CHUNKS)])
        for n in range(len(GROUPS)):
            wait_all(mean_send.at[n], arrived[n].at[pl.ds(1, grps - 1)])
        wait_all(spec_send, spec_in.at[pl.ds(1, tiles - 1)])


def fused(visibility, dish_pair_okay, triangles):
    block, dishes, channels = visibility.shape[1:]
    tiles = lax.axis_size("tile")
    grps = lax.axis_size("grp")
    f32, bf16, i32 = jnp.float32, jnp.bfloat16, jnp.int32
    groups = len(GROUPS)
    dma = pltpu.SemaphoreType.DMA
    return pl.pallas_call(
        kernel,
        out_shape=(
            jax.ShapeDtypeStruct((2, LEVELS * TRI_LVL), f32),
            jax.ShapeDtypeStruct((2, channels), f32),
        ),
        in_specs=[pl.BlockSpec(memory_space=pltpu.HBM)] * 3,
        out_specs=(pl.BlockSpec(memory_space=pltpu.VMEM), pl.BlockSpec(memory_space=pltpu.VMEM)),
        scratch_shapes=[
            pltpu.VMEM((2, block, dishes, channels), bf16),
            pltpu.VMEM((block, dishes), i32),
            pltpu.VMEM((3, LEVELS * TRI_LVL), i32),
            pltpu.VMEM((block, dishes, channels), bf16),
            pltpu.VMEM((block * dishes, 2, channels), f32),
            pltpu.VMEM((LEVELS, 1, TRI_LVL), i32),
            pltpu.VMEM((1, LEVELS * TRI_LVL), i32),
            pltpu.SMEM((1, TRI_LVL), i32),
            pltpu.SMEM((1, TRI_LVL), i32),
            pltpu.SMEM((1, LEVELS * TRI_LVL), i32),
            pltpu.VMEM((block * block, 2 * channels), bf16),
            pltpu.VMEM((LEVELS, CHUNKS, CHUNK, 2 * channels), f32),
            pltpu.VMEM((2 * CHUNK, channels), f32),
            pltpu.VMEM((LEVELS, 2 * TRI_LVL, channels), f32),
            pltpu.VMEM((PIECES, 2, CHUNK, channels), bf16),
            pltpu.VMEM((PIECES, 2, CHUNK, channels), bf16),
            pltpu.VMEM((CHUNKS, 2 * CHUNK, 2 * channels), bf16),
            pltpu.VMEM((4, channels), f32),
            pltpu.VMEM((tiles, 4, channels), f32),
            [pltpu.VMEM((count, 2 * CHUNK), f32) for _, count in GROUPS],
            [pltpu.VMEM((grps, count, 2 * CHUNK), f32) for _, count in GROUPS],
            pltpu.SemaphoreType.REGULAR((3,)),
            dma((2,)), dma((block // ROWS,)), dma,
            dma((LEVELS,)), dma((LEVELS,)),
            dma((LEVELS,)), dma((CHUNKS + 1,)),
            dma((groups,)), dma((groups,)),
            dma, dma,
        ],
        compiler_params=pltpu.CompilerParams(
            collective_id=0, has_side_effects=True, vmem_limit_bytes=48 * 2**20
        ),
        name="closure",
    )(*(pltpu.with_memory_space_constraint(x, pltpu.HBM) for x in (visibility, dish_pair_okay, triangles)))


def body(visibility, dish_pair_okay, triangles):
    means, closure = fused(visibility, dish_pair_okay, triangles)
    tile = lax.axis_index("tile")
    width = closure.shape[1] // lax.axis_size("tile")
    return means, lax.dynamic_slice(closure, (0, tile * width), (2, width))


def solution(mesh):
    placed = (P(None, "tile", None, "grp"), P("tile", None), P(None, "tile"))
    return jax.shard_map(
        body,
        mesh=mesh,
        in_specs=placed,
        out_specs=(P(None, "tile"), P(None, ("grp", "tile"))),
        check_vma=False,
    )
```

time: 36.8 us -> 31.2 us (0.85)
  Pallas kernels: 33.4 us -> 29.1 us
  local copies, waits for them, and re-layouts: 2.62 us -> 1.24 us
    pallas_call x1, Pallas kernels: 33.4 us -> 29.1 us  [fused(): pl.pallas_call(kernel, out_shape=(jax.ShapeDtypeStruct((2, LEVELS * TRI_L...]
    unnamed x1, local copies, waits for them, and re-layouts: 1.32 us -> 0.6 us
    dynamic_slice x1, local copies, waits for them, and re-layouts: 1.29 us -> 0.64 us  [body(): return (means, lax.dynamic_slice(closure, (0, tile * width), (2, width)))]
where the time goes in v4:
time: 31.2 us; the launch traced here: 31 us
  Pallas kernels  29.1 us (93%)
  local copies, waits for them, and re-layouts  1.24 us (4%)
  between operations  0.64 us (2%)
    pallas_call x1, Pallas kernels, fused(): pl.pallas_call(kernel, out_shape=(jax.ShapeDtypeStruct((2, LEVELS * TRI_L...  29.1 us
    dynamic_slice x1, local copies, waits for them, and re-layouts, body(): return (means, lax.dynamic_slice(closure, (0, tile * width), (2, width)))  0.64 us

profile of v4, /device:TPU:1, one launch (start us, length us, event | category | flops | bytes accessed | tf_op | source)
XLA Modules:
  0.0 31.0 jit_solution(5295423320435728947)
XLA Ops:
  0.6 29.1 %closure.1 = (f32[2,2048]{1,0:T(2,128)S(1)}, f32[2,128]{1,0:T(2,128)S(1)}) custom-call(bf16[2,16,512,128]{3,2,1,0:T(8,128)(2,1)} %vis_hbm.1, s32[16,512]{1,0:T(8,128)} %okay_hbm.1, s32[3,2048]{1,0:T(4,128)} %tri_hbm.1), custom_call_target="tpu_custom_call" | custom-call | tf_op jit(solution)/shard_map/closure/pallas_call | solution.py:297
  29.8 0.6 %constant_dynamic-slice_fusion = f32[2,4]{1,0:T(2,128)} fusion(f32[2,128]{1,0:T(2,128)S(1)} %get-tuple-element.5, s32[]{:T(128)S(6)} %select_n.3), kind=kLoop, calls=%fused_computation | loop fusion | bytes 68 | tf_op jit(solution)/shard_map/dynamic_slice | solution.py:345
  30.4 0.6 %copy.6 = f32[2,2048]{1,0:T(2,128)} copy(f32[2,2048]{1,0:T(2,128)S(1)} %get-tuple-element.8) | data formatting | bytes 32768

commit v5 on v4

--- a/solution.py
+++ b/solution.py
@@ -14,6 +14,7 @@
 UNROLL = 32
 ROWS = 4
 MESH = pl.DeviceIdType.MESH
+ACROSS = ((1, 0, 0, 0), (-1, 0, 0, 0), (0, 0, 1, 0), (0, 0, -1, 0))
 NEAR = ((1, 0, 0, 0), (-1, 0, 0, 0), (0, 1, 0, 0), (0, -1, 0, 0), (0, 0, 1, 0), (0, 0, -1, 0), (0, 0, 0, 1))
 SECOND = ((0, 0, 0, 1), (2, 0, 0, 0), (0, 2, 0, 0), (0, 0, 2, 0), (0, 0, -2, 0))
 THIRD = ((0, 0, 2, 0), (0, 0, -2, 0))
@@ -47,13 +48,29 @@
     barrier = pltpu.get_barrier_semaphore()
     spots = (lax.rem(grp, 4), lax.rem(lax.div(tile, 2), 4), lax.div(grp, 4) * 4 + lax.div(tile, 8), lax.rem(tile, 2))
 
+    def there(step):
+        x, y, z, core = (lax.rem(at + d + n, n) for at, d, n in zip(spots, step, (4, 4, 8, 2)))
+        return {"grp": lax.div(z, 4) * 4 + x, "tile": lax.rem(z, 4) * 8 + y * 2 + core}, (x, y, z)
+
     def tell(sem, steps):
         for step in steps:
-            x, y, z, core = (lax.rem(at + d + n, n) for at, d, n in zip(spots, step, (4, 4, 8, 2)))
-            there = {"grp": lax.div(z, 4) * 4 + x, "tile": lax.rem(z, 4) * 8 + y * 2 + core}
-            pl.semaphore_signal(sem, inc=1, device_id=there, device_id_type=MESH)
-
-    tell(barrier, NEAR)
+            pl.semaphore_signal(sem, inc=1, device_id=there(step)[0], device_id_type=MESH)
+
+    odd = lax.rem(spots[1], 2)
+    pair_step = (0, 1 - 2 * odd, 0, 0)
+    cross_step = (0, 2 * odd - 1, 0, 0)
+    across = []
+    for step, line in ((ACROSS[0], 0), (ACROSS[1], 0), (ACROSS[2], 2), (ACROSS[3], 2), (cross_step, 1)):
+        device, place = there(step)
+        across.append((device, place[line] > spots[line]))
+    higher = sum(jnp.where(up, 1, 0) for _, up in across)
+    tell(barrier, ((0, 0, 0, 1), pair_step))
+    for device, up in across:
+
+        @pl.when(up)
+        def greet():
+            pl.semaphore_signal(barrier, inc=1, device_id=device, device_id_type=MESH)
+
     partner = [tile + 1 - 2 * lax.rem(tile, 2), tile + 2 - 4 * lax.rem(lax.div(tile, 2), 2)]
 
     with jax.named_scope("tri_wait"):
@@ -68,8 +85,13 @@
         ask[lvl] = wanted[:, lvl * TRI_LVL : (lvl + 1) * TRI_LVL]
 
     with jax.named_scope("barrier"):
-        pl.semaphore_wait(barrier, len(NEAR))
-    tell(known.at[0], NEAR)
+        pl.semaphore_wait(barrier, 2 + len(across) - higher)
+    for device, up in across:
+
+        @pl.when(jnp.logical_not(up))
+        def answer():
+            pl.semaphore_signal(known.at[0], inc=1, device_id=device, device_id_type=MESH)
+
     asks = []
     for lvl in range(LEVELS):
         asks.append(
@@ -209,20 +231,24 @@
     rows = [None] * LEVELS
     with jax.named_scope("serve1"):
         rows[1] = [serve(1, c) for c in range(CHUNKS)]
-    with jax.named_scope("known0"):
-        pl.semaphore_wait(known.at[0], len(NEAR))
-    tell(known.at[1], SECOND)
     asks[0].wait_recv()
     with jax.named_scope("serve0"):
         rows[0] = [serve(0, c) for c in range(CHUNKS)]
+    with jax.named_scope("known0"):
+
+        @pl.when(higher > 0)
+        def answered():
+            pl.semaphore_wait(known.at[0], higher)
+
+    tell(known.at[1], NEAR)
     to_pr.wait()
     zero = jnp.zeros((8, channels), f32)
     sums = (zero, zero, zero)
     with jax.named_scope("own0"):
         own(0)
     with jax.named_scope("known1"):
-        pl.semaphore_wait(known.at[1], len(SECOND))
-    tell(known.at[2], THIRD)
+        pl.semaphore_wait(known.at[1], len(NEAR))
+    tell(known.at[2], SECOND)
     with jax.named_scope("rows0"):
         wait_all(row_recv.at[CHUNKS], got.at[pl.ds(0, CHUNKS)])
     with jax.named_scope("combine0"):
@@ -230,10 +256,13 @@
         total = lanes(0, 0)
         for c in range(1, CHUNKS):
             total = total + lanes(c, c)
+    with jax.named_scope("known2"):
+        pl.semaphore_wait(known.at[2], len(SECOND))
+    tell(known.at[3], THIRD)
     with jax.named_scope("own1"):
         own(1)
-    with jax.named_scope("known2"):
-        pl.semaphore_wait(known.at[2], len(THIRD))
+    with jax.named_scope("known3"):
+        pl.semaphore_wait(known.at[3], len(THIRD))
     with jax.named_scope("share"):
         share(0, total)
     for n, (start, count) in enumerate(GROUPS[1:], 1):
@@ -249,13 +278,17 @@
             share(n, total)
 
     with jax.named_scope("spec_send"):
-        for k in range(3):
-            spec[k : k + 1, :] = jnp.sum(sums[k], axis=0, keepdims=True)
-        spec[3:4, :] = jnp.zeros((1, channels), f32)
-        spec_in[0] = spec[...]
+        width = channels // tiles
+        row = lax.broadcasted_iota(jnp.int32, (tiles, channels), 0)
+        lane = lax.broadcasted_iota(jnp.int32, (tiles, channels), 1)
+        mine = jnp.logical_and(lane >= row * width, lane < (row + 1) * width)
+        packed = [jnp.where(mine, jnp.sum(x, axis=0, keepdims=True), 0.0) for x in sums]
+        packed = packed[0] + pltpu.roll(packed[1], channels // 4, 1) + pltpu.roll(packed[2], channels // 2, 1)
+        spec.reshape(tiles, channels)[...] = packed
+        spec_in[0] = spec[tile]
         for k in range(1, tiles):
             send = pltpu.make_async_remote_copy(
-                src_ref=spec, dst_ref=spec_in.at[k],
+                src_ref=spec.at[lax.rem(tile + k, tiles)], dst_ref=spec_in.at[k],
                 send_sem=spec_send, recv_sem=spec_recv,
                 device_id={"tile": lax.rem(tile + k, tiles)}, device_id_type=MESH,
             )
@@ -276,7 +309,9 @@
     with jax.named_scope("spec_wait"):
         wait_all(spec_recv, spec_in.at[pl.ds(1, tiles - 1)])
         total = jnp.sum(spec_in[...], axis=0)
-        closure_ref[...] = total[0:2] / (1.0 + total[2:3])
+        norm = 1.0 + pltpu.roll(total, channels // 2, 1)
+        closure_ref[0:1] = total / norm
+        closure_ref[1:2] = pltpu.roll(total, channels - channels // 4, 1) / norm
 
     with jax.named_scope("send_wait"):
         for lvl in range(LEVELS):
@@ -320,11 +355,11 @@
             pltpu.VMEM((PIECES, 2, CHUNK, channels), bf16),
             pltpu.VMEM((PIECES, 2, CHUNK, channels), bf16),
             pltpu.VMEM((CHUNKS, 2 * CHUNK, 2 * channels), bf16),
-            pltpu.VMEM((4, channels), f32),
-            pltpu.VMEM((tiles, 4, channels), f32),
+            pltpu.VMEM((tiles, 1, channels), f32),
+            pltpu.VMEM((tiles, 1, channels), f32),
             [pltpu.VMEM((count, 2 * CHUNK), f32) for _, count in GROUPS],
             [pltpu.VMEM((grps, count, 2 * CHUNK), f32) for _, count in GROUPS],
-            pltpu.SemaphoreType.REGULAR((3,)),
+            pltpu.SemaphoreType.REGULAR((4,)),
             dma((2,)), dma((block // ROWS,)), dma,
             dma((LEVELS,)), dma((LEVELS,)),
             dma((LEVELS,)), dma((CHUNKS + 1,)),

time: 31.2 us -> 30.7 us (0.984)
  the two profiles are of different devices: /device:TPU:1 before, /device:TPU:16 now
where the time goes in v5:
time: 30.7 us; the launch traced here: 30.6 us
  Pallas kernels  28.7 us (93%)
  local copies, waits for them, and re-layouts  1.24 us (4%)
  between operations  0.64 us (2%)
    pallas_call x1, Pallas kernels, fused(): pl.pallas_call(kernel, out_shape=(jax.ShapeDtypeStruct((2, LEVELS * TRI_L...  28.7 us
    dynamic_slice x1, local copies, waits for them, and re-layouts, body(): return (means, lax.dynamic_slice(closure, (0, tile * width), (2, width)))  0.64 us

profile of v5, /device:TPU:16, one launch (start us, length us, event | category | flops | bytes accessed | tf_op | source)
XLA Modules:
  0.0 30.6 jit_solution(2787200188648735611)
XLA Ops:
  0.6 28.7 %closure.1 = (f32[2,2048]{1,0:T(2,128)S(1)}, f32[2,128]{1,0:T(2,128)S(1)}) custom-call(bf16[2,16,512,128]{3,2,1,0:T(8,128)(2,1)} %vis_hbm.1, s32[16,512]{1,0:T(8,128)} %okay_hbm.1, s32[3,2048]{1,0:T(4,128)} %tri_hbm.1), custom_call_target="tpu_custom_call" | custom-call | tf_op jit(solution)/shard_map/closure/pallas_call | solution.py:332
  29.3 0.6 %constant_dynamic-slice_fusion = f32[2,4]{1,0:T(2,128)} fusion(f32[2,128]{1,0:T(2,128)S(1)} %get-tuple-element.5, s32[]{:T(128)S(6)} %select_n.3), kind=kLoop, calls=%fused_computation | loop fusion | bytes 68 | tf_op jit(solution)/shard_map/dynamic_slice | solution.py:380
  29.9 0.6 %copy.6 = f32[2,2048]{1,0:T(2,128)} copy(f32[2,2048]{1,0:T(2,128)S(1)} %get-tuple-element.8) | data formatting | bytes 32768

commit v6 on v5

--- a/solution.py
+++ b/solution.py
@@ -73,10 +73,10 @@
 
     partner = [tile + 1 - 2 * lax.rem(tile, 2), tile + 2 - 4 * lax.rem(lax.div(tile, 2), 2)]
 
+    for k in range(block // ROWS):
+        load_rows(k).start()
     with jax.named_scope("tri_wait"):
         load_tri.wait()
-    for k in range(block // ROWS):
-        load_rows(k).start()
     first = jnp.bitwise_and(tri[0:1, :], block - 1)
     second = jnp.bitwise_and(tri[1:2, :], block - 1)
     third = tri[2:3, :]

time: 30.7 us -> 30 us (0.977)
  the two profiles are of different devices: /device:TPU:16 before, /device:TPU:1 now
where the time goes in v6:
time: 30 us; the launch traced here: 29.6 us
  Pallas kernels  27.7 us (92%)
  local copies, waits for them, and re-layouts  1.24 us (4%)
  between operations  0.64 us (2%)
    pallas_call x1, Pallas kernels, fused(): pl.pallas_call(kernel, out_shape=(jax.ShapeDtypeStruct((2, LEVELS * TRI_L...  27.7 us
    dynamic_slice x1, local copies, waits for them, and re-layouts, body(): return (means, lax.dynamic_slice(closure, (0, tile * width), (2, width)))  0.64 us
    unnamed x1, local copies, waits for them, and re-layouts  0.6 us

profile of v6, /device:TPU:1, one launch (start us, length us, event | category | flops | bytes accessed | tf_op | source)
XLA Modules:
  0.0 29.6 jit_solution(8304173913514175525)
XLA Ops:
  0.6 27.7 %closure.1 = (f32[2,2048]{1,0:T(2,128)S(1)}, f32[2,128]{1,0:T(2,128)S(1)}) custom-call(bf16[2,16,512,128]{3,2,1,0:T(8,128)(2,1)} %vis_hbm.1, s32[16,512]{1,0:T(8,128)} %okay_hbm.1, s32[3,2048]{1,0:T(4,128)} %tri_hbm.1), custom_call_target="tpu_custom_call" | custom-call | tf_op jit(solution)/shard_map/closure/pallas_call | solution.py:332
  28.4 0.6 %constant_dynamic-slice_fusion = f32[2,4]{1,0:T(2,128)} fusion(f32[2,128]{1,0:T(2,128)S(1)} %get-tuple-element.5, s32[]{:T(128)S(6)} %select_n.3), kind=kLoop, calls=%fused_computation | loop fusion | bytes 68 | tf_op jit(solution)/shard_map/dynamic_slice | solution.py:380
  29.0 0.6 %copy.6 = f32[2,2048]{1,0:T(2,128)} copy(f32[2,2048]{1,0:T(2,128)S(1)} %get-tuple-element.8) | data formatting | bytes 32768

commit v7 on v6

--- a/solution.py
+++ b/solution.py
@@ -84,6 +84,9 @@
     for lvl in range(LEVELS):
         ask[lvl] = wanted[:, lvl * TRI_LVL : (lvl + 1) * TRI_LVL]
 
+    with jax.named_scope("okay"):
+        load_okay.wait()
+        flags_t = jnp.transpose(okay[...].astype(f32)).astype(bf16)
     with jax.named_scope("barrier"):
         pl.semaphore_wait(barrier, 2 + len(across) - higher)
     for device, up in across:
@@ -103,14 +106,8 @@
         )
     asks[1].start()
     asks[0].start()
-    own_pr[...] = first * dishes + third
-    to_pr = pltpu.make_async_copy(own_pr, s_pr, smem_sem)
-    to_pr.start()
-    pair = (first * block + second).astype(f32)
 
     with jax.named_scope("flags"):
-        load_okay.wait()
-        flags_t = jnp.transpose(okay[...].astype(f32)).astype(bf16)
         for c in range(0, block, 2):
             row = lax.broadcasted_iota(jnp.int32, (block, 2 * channels), 0)
             col = lax.broadcasted_iota(jnp.int32, (block, 2 * channels), 1)
@@ -133,6 +130,10 @@
         for k in range(block // ROWS):
             load_rows(k).wait()
             lax.fori_loop(k * ROWS, (k + 1) * ROWS, build, 0)
+    own_pr[...] = first * dishes + third
+    to_pr = pltpu.make_async_copy(own_pr, s_pr, smem_sem)
+    to_pr.start()
+    pair = (first * block + second).astype(f32)
     with jax.named_scope("ask_wait"):
         asks[1].wait_recv()
 
@@ -228,27 +229,40 @@
             )
             send.start()
 
+    half = lax.div(spots[2], 4)
+
+    def relay(turn, stage):
+        @pl.when(turn == 1)
+        def pass_on():
+            if stage == 0:
+
+                @pl.when(higher > 0)
+                def answered():
+                    pl.semaphore_wait(known.at[0], higher)
+
+                tell(known.at[1], NEAR)
+            elif stage == 1:
+                pl.semaphore_wait(known.at[1], len(NEAR))
+                tell(known.at[2], SECOND)
+            else:
+                pl.semaphore_wait(known.at[2], len(SECOND))
+                tell(known.at[3], THIRD)
+
     rows = [None] * LEVELS
     with jax.named_scope("serve1"):
         rows[1] = [serve(1, c) for c in range(CHUNKS)]
+    relay(half, 0)
     asks[0].wait_recv()
     with jax.named_scope("serve0"):
         rows[0] = [serve(0, c) for c in range(CHUNKS)]
-    with jax.named_scope("known0"):
-
-        @pl.when(higher > 0)
-        def answered():
-            pl.semaphore_wait(known.at[0], higher)
-
-    tell(known.at[1], NEAR)
+    relay(half, 1)
     to_pr.wait()
     zero = jnp.zeros((8, channels), f32)
     sums = (zero, zero, zero)
     with jax.named_scope("own0"):
         own(0)
-    with jax.named_scope("known1"):
-        pl.semaphore_wait(known.at[1], len(NEAR))
-    tell(known.at[2], SECOND)
+    relay(half, 2)
+    relay(1 - half, 0)
     with jax.named_scope("rows0"):
         wait_all(row_recv.at[CHUNKS], got.at[pl.ds(0, CHUNKS)])
     with jax.named_scope("combine0"):
@@ -256,11 +270,10 @@
         total = lanes(0, 0)
         for c in range(1, CHUNKS):
             total = total + lanes(c, c)
-    with jax.named_scope("known2"):
-        pl.semaphore_wait(known.at[2], len(SECOND))
-    tell(known.at[3], THIRD)
+    relay(1 - half, 1)
     with jax.named_scope("own1"):
         own(1)
+    relay(1 - half, 2)
     with jax.named_scope("known3"):
         pl.semaphore_wait(known.at[3], len(THIRD))
     with jax.named_scope("share"):

time: 30 us -> 30.1 us (level)
  no operation moved by 1% of the time
where the time goes in v7:
time: 30.1 us; the launch traced here: 29.6 us
  Pallas kernels  27.8 us (92%)
  local copies, waits for them, and re-layouts  1.24 us (4%)
  between operations  0.64 us (2%)
    pallas_call x1, Pallas kernels, fused(): pl.pallas_call(kernel, out_shape=(jax.ShapeDtypeStruct((2, LEVELS * TRI_L...  27.8 us
    dynamic_slice x1, local copies, waits for them, and re-layouts, body(): return (means, lax.dynamic_slice(closure, (0, tile * width), (2, width)))  0.64 us
    unnamed x1, local copies, waits for them, and re-layouts  0.6 us

profile of v7, /device:TPU:1, one launch (start us, length us, event | category | flops | bytes accessed | tf_op | source)
XLA Modules:
  0.0 29.6 jit_solution(10639768764276828239)
XLA Ops:
  0.6 27.8 %closure.1 = (f32[2,2048]{1,0:T(2,128)S(1)}, f32[2,128]{1,0:T(2,128)S(1)}) custom-call(bf16[2,16,512,128]{3,2,1,0:T(8,128)(2,1)} %vis_hbm.1, s32[16,512]{1,0:T(8,128)} %okay_hbm.1, s32[3,2048]{1,0:T(4,128)} %tri_hbm.1), custom_call_target="tpu_custom_call" | custom-call | tf_op jit(solution)/shard_map/closure/pallas_call | solution.py:345
  28.4 0.6 %constant_dynamic-slice_fusion = f32[2,4]{1,0:T(2,128)} fusion(f32[2,128]{1,0:T(2,128)S(1)} %get-tuple-element.5, s32[]{:T(128)S(6)} %select_n.3), kind=kLoop, calls=%fused_computation | loop fusion | bytes 68 | tf_op jit(solution)/shard_map/dynamic_slice | solution.py:393
  29.0 0.6 %copy.6 = f32[2,2048]{1,0:T(2,128)} copy(f32[2,2048]{1,0:T(2,128)S(1)} %get-tuple-element.8) | data formatting | bytes 32768

commit v8 on v6

--- a/solution.py
+++ b/solution.py
@@ -84,6 +84,9 @@
     for lvl in range(LEVELS):
         ask[lvl] = wanted[:, lvl * TRI_LVL : (lvl + 1) * TRI_LVL]
 
+    with jax.named_scope("okay"):
+        load_okay.wait()
+        flags_t = jnp.transpose(okay[...].astype(f32)).astype(bf16)
     with jax.named_scope("barrier"):
         pl.semaphore_wait(barrier, 2 + len(across) - higher)
     for device, up in across:
@@ -103,14 +106,8 @@
         )
     asks[1].start()
     asks[0].start()
-    own_pr[...] = first * dishes + third
-    to_pr = pltpu.make_async_copy(own_pr, s_pr, smem_sem)
-    to_pr.start()
-    pair = (first * block + second).astype(f32)
 
     with jax.named_scope("flags"):
-        load_okay.wait()
-        flags_t = jnp.transpose(okay[...].astype(f32)).astype(bf16)
         for c in range(0, block, 2):
             row = lax.broadcasted_iota(jnp.int32, (block, 2 * channels), 0)
             col = lax.broadcasted_iota(jnp.int32, (block, 2 * channels), 1)
@@ -133,6 +130,10 @@
         for k in range(block // ROWS):
             load_rows(k).wait()
             lax.fori_loop(k * ROWS, (k + 1) * ROWS, build, 0)
+    own_pr[...] = first * dishes + third
+    to_pr = pltpu.make_async_copy(own_pr, s_pr, smem_sem)
+    to_pr.start()
+    pair = (first * block + second).astype(f32)
     with jax.named_scope("ask_wait"):
         asks[1].wait_recv()
 

time: 30 us -> 30 us (level)
  no operation moved by 1% of the time
where the time goes in v8:
time: 30 us; the launch traced here: 29.6 us
  Pallas kernels  27.7 us (92%)
  local copies, waits for them, and re-layouts  1.24 us (4%)
  between operations  0.64 us (2%)
    pallas_call x1, Pallas kernels, fused(): pl.pallas_call(kernel, out_shape=(jax.ShapeDtypeStruct((2, LEVELS * TRI_L...  27.7 us
    dynamic_slice x1, local copies, waits for them, and re-layouts, body(): return (means, lax.dynamic_slice(closure, (0, tile * width), (2, width)))  0.64 us
    unnamed x1, local copies, waits for them, and re-layouts  0.6 us

profile of v8, /device:TPU:1, one launch (start us, length us, event | category | flops | bytes accessed | tf_op | source)
XLA Modules:
  0.0 29.6 jit_solution(14907650567113823963)
XLA Ops:
  0.6 27.7 %closure.1 = (f32[2,2048]{1,0:T(2,128)S(1)}, f32[2,128]{1,0:T(2,128)S(1)}) custom-call(bf16[2,16,512,128]{3,2,1,0:T(8,128)(2,1)} %vis_hbm.1, s32[16,512]{1,0:T(8,128)} %okay_hbm.1, s32[3,2048]{1,0:T(4,128)} %tri_hbm.1), custom_call_target="tpu_custom_call" | custom-call | tf_op jit(solution)/shard_map/closure/pallas_call | solution.py:333
  28.4 0.6 %constant_dynamic-slice_fusion = f32[2,4]{1,0:T(2,128)} fusion(f32[2,128]{1,0:T(2,128)S(1)} %get-tuple-element.5, s32[]{:T(128)S(6)} %select_n.3), kind=kLoop, calls=%fused_computation | loop fusion | bytes 68 | tf_op jit(solution)/shard_map/dynamic_slice | solution.py:381
  29.0 0.6 %copy.6 = f32[2,2048]{1,0:T(2,128)} copy(f32[2,2048]{1,0:T(2,128)S(1)} %get-tuple-element.8) | data formatting | bytes 32768
